TPU v7x, 128 devices: a whole 4x4x4 slice. The times are simulated.
128 devices in a mesh: dp: 4 (over x_lo, core), ctx: 32 (over z, y, x_hi).
Axes of the slice: x: 4 (x_hi: 2, x_lo: 2; x = x_hi * 2 + x_lo), y: 4, z: 4, core: 2. Of those that a mesh axis runs over, the one named last changes fastest.
Arguments:
- queries: bfloat16 [16384, 4096], P(('dp', 'ctx')), may hold values from -6 to 6
- key_proj: bfloat16 [16384, 512], P(('dp', 'ctx')), may hold values from -6 to 6
- value_proj: bfloat16 [16384, 512], P(('dp', 'ctx')), may hold values from -6 to 6
- out_grad: bfloat16 [16384, 4096], P(('dp', 'ctx')), may hold values from -6 to 6
- row_plan: int32 [16384], P(('dp', 'ctx')), may hold values from 0 to 127, as said below
- segments: int32 [4, 4096], P('dp', 'ctx'), may hold values from 0 to 5, as said below
Outputs:
- attended: bfloat16 [16384, 4096], P(('dp', 'ctx'))
- query_grad: bfloat16 [16384, 4096], P(('dp', 'ctx'))
- key_grad: bfloat16 [16384, 512], P(('dp', 'ctx'))
- value_grad: bfloat16 [16384, 512], P(('dp', 'ctx'))
Inputs may be any that keep to these rules, and one draw needn't show every extreme that they name: `row_plan`: each aligned block of 128 entries (the rows of one device) is a permutation of 0 to 127. `segments`: along each row the ids never fall, and every id from 0 to 5 occurs. Every document has at most 2176 positions, and in each row one document has exactly that many.
All inputs are finite; a program needn't handle non-finite values.
Results may differ from a plain program's by a relative error of at most 0.0083.
Values may be sent and summed in bfloat16 or wider, within the bound.
No kernel may reach another device: no remote copies, remote signals or barrier semaphores. Data moves between devices by JAX's collectives and lax.ppermute only.
A program may use at most 128 MiB of HBM per device.

v0:
```python
import jax
import jax.numpy as jnp
from jax import lax
from jax.sharding import PartitionSpec as P

HEADS = 32
KV_HEADS = 4
HEAD_DIM = 128


NEG = -1e30


def sent_together(arrays, axis, split_dim, concat_dim, along):
    ends, at = ([], 0)
    for a in arrays[:-1]:
        at += a.shape[along]
        ends.append(at)
    both = jnp.concatenate(arrays, axis=along)
    return tuple(
        jnp.split(
            lax.all_to_all(both, axis, split_axis=split_dim, concat_axis=concat_dim, tiled=True),
            ends,
            axis=along,
        )
    )


def in_one_piece(arrays, axis, dim, along):
    ends, at = ([], 0)
    for a in arrays[:-1]:
        at += a.shape[along]
        ends.append(at)
    both = jnp.concatenate(arrays, axis=along)
    return tuple(jnp.split(lax.all_gather(both, axis, axis=dim, tiled=True), ends, axis=along))


def passed_along(value, axis, steps):
    count = lax.axis_size(axis)
    first, last = (max(0, -steps), min(count, count - steps))
    return lax.ppermute(value, axis, [(source, source + steps) for source in range(first, last)])


def block_scores(q_heads, key_blk, seg_rows, pos_rows, seg_keys, pos_keys, scaling):
    raw_scores = (
        jnp.einsum("qkgd,skd->kgqs", q_heads, key_blk, preferred_element_type=jnp.float32) * scaling
    )
    visible = (seg_keys[None, :] == seg_rows[:, None]) & (pos_keys[None, :] <= pos_rows[:, None])
    return (jnp.where(visible, raw_scores, NEG), visible)


def on_device(queries, key_proj, value_proj, out_grad, row_plan, segments):
    rows_here = queries.shape[0]
    groups = HEADS // KV_HEADS
    scaling = HEAD_DIM ** (-0.5)
    inverse = jnp.zeros_like(row_plan).at[row_plan].set(jnp.arange(rows_here, dtype=jnp.int32))
    q_rows, k_rows, v_rows, d_rows = sent_together(
        (queries[row_plan], key_proj[row_plan], value_proj[row_plan], out_grad[row_plan]),
        "dp",
        0,
        0,
        1,
    )
    k_all, v_all, seg_all = (
        *in_one_piece((k_rows, v_rows), "ctx", 0, 1),
        lax.all_gather(segments, "ctx", axis=1, tiled=True),
    )
    seq_len = k_all.shape[0]
    block_len = min(512, seq_len)
    blocks = seq_len // block_len
    my_index = lax.axis_index("ctx")
    first_row = my_index * rows_here
    last_row = first_row + rows_here - 1
    pos_rows = first_row + jnp.arange(rows_here, dtype=jnp.int32)
    seg_rows = segments[0]
    q_heads = q_rows.reshape(rows_here, KV_HEADS, groups, HEAD_DIM)

    def cut_block(keys_all, vals_all, seg_keys_all, block_idx):
        offset = block_idx * block_len
        key_blk = lax.dynamic_slice_in_dim(keys_all, offset, block_len, 0).reshape(
            block_len, KV_HEADS, HEAD_DIM
        )
        val_blk = lax.dynamic_slice_in_dim(vals_all, offset, block_len, 0).reshape(
            block_len, KV_HEADS, HEAD_DIM
        )
        seg_keys = lax.dynamic_slice_in_dim(seg_keys_all, offset, block_len, 0)
        pos_keys = offset + jnp.arange(block_len, dtype=jnp.int32)
        is_live = (offset <= last_row) & (seg_keys[block_len - 1] >= seg_rows[0])
        return (key_blk, val_blk, seg_keys, pos_keys, is_live, offset)

    seg_fwd = seg_all[0]

    def stats_step(block_idx, running):
        key_blk, val_blk, seg_keys, pos_keys, is_live, offset = cut_block(
            k_all, v_all, seg_fwd, block_idx
        )

        def stats_compute(running):
            row_top, row_sum = running
            scores, visible = block_scores(
                q_heads, key_blk, seg_rows, pos_rows, seg_keys, pos_keys, scaling
            )
            new_top = jnp.maximum(row_top, jnp.max(scores, axis=3))
            fresh = jnp.sum(jnp.where(visible, jnp.exp(scores - new_top[..., None]), 0.0), axis=3)
            return (new_top, row_sum * jnp.exp(row_top - new_top) + fresh)

        return lax.cond(is_live, stats_compute, lambda running: running, running)

    stat_shape = (KV_HEADS, groups, rows_here)
    row_top, row_sum = lax.fori_loop(
        0,
        blocks,
        stats_step,
        (jnp.full(stat_shape, NEG, jnp.float32), jnp.zeros(stat_shape, jnp.float32)),
    )
    log_sum = row_top + jnp.log(row_sum)

    def output_step(block_idx, running):
        key_blk, val_blk, seg_keys, pos_keys, is_live, offset = cut_block(
            k_all, v_all, seg_fwd, block_idx
        )

        def output_compute(running):
            scores, visible = block_scores(
                q_heads, key_blk, seg_rows, pos_rows, seg_keys, pos_keys, scaling
            )
            weights = jnp.where(visible, jnp.exp(scores - log_sum[..., None]), 0.0).astype(
                jnp.bfloat16
            )
            return running + jnp.einsum(
                "kgqs,skd->qkgd", weights, val_blk, preferred_element_type=jnp.float32
            )

        return lax.cond(is_live, output_compute, lambda running: running, running)

    out = lax.fori_loop(
        0, blocks, output_step, jnp.zeros((rows_here, KV_HEADS, groups, HEAD_DIM), jnp.float32)
    )
    back_out = lax.all_to_all(
        out.astype(jnp.bfloat16).reshape(rows_here, -1),
        "dp",
        split_axis=0,
        concat_axis=0,
        tiled=True,
    )
    attended = back_out[inverse]
    d_heads = d_rows.reshape(rows_here, KV_HEADS, groups, HEAD_DIM)
    row_dot = jnp.transpose(jnp.sum(d_heads.astype(jnp.float32) * out, axis=3), (1, 2, 0))
    back_k, back_v, back_seg = (
        *in_one_piece((k_rows, v_rows), "ctx", 0, 1),
        lax.all_gather(segments, "ctx", axis=1, tiled=True),
    )
    seg_bwd = back_seg[0]

    def grad_step(block_idx, running):
        key_blk, val_blk, seg_keys, pos_keys, is_live, offset = cut_block(
            back_k, back_v, seg_bwd, block_idx
        )

        def grad_compute(running):
            q_grad, k_term, v_term = running
            scores, visible = block_scores(
                q_heads, key_blk, seg_rows, pos_rows, seg_keys, pos_keys, scaling
            )
            probs = jnp.where(visible, jnp.exp(scores - log_sum[..., None]), 0.0)
            weights = probs.astype(jnp.bfloat16)
            dprobs = jnp.einsum(
                "qkgd,skd->kgqs", d_heads, val_blk, preferred_element_type=jnp.float32
            )
            dscore = (probs * (dprobs - row_dot[..., None]) * scaling).astype(jnp.bfloat16)
            q_grad = q_grad + jnp.einsum(
                "kgqs,skd->qkgd", dscore, key_blk, preferred_element_type=jnp.float32
            )
            k_part = jnp.einsum(
                "kgqs,qkgd->skd", dscore, q_heads, preferred_element_type=jnp.float32
            )
            v_part = jnp.einsum(
                "kgqs,qkgd->skd", weights, d_heads, preferred_element_type=jnp.float32
            )
            k_term = lax.dynamic_update_slice_in_dim(k_term, k_part, offset, 0)
            v_term = lax.dynamic_update_slice_in_dim(v_term, v_part, offset, 0)
            return (q_grad, k_term, v_term)

        return lax.cond(is_live, grad_compute, lambda running: running, running)

    term_zeros = jnp.zeros((seq_len, KV_HEADS, HEAD_DIM), jnp.float32)
    q_grad, k_term, v_term = lax.fori_loop(
        0,
        blocks,
        grad_step,
        (jnp.zeros((rows_here, KV_HEADS, groups, HEAD_DIM), jnp.float32), term_zeros, term_zeros),
    )
    k_term = k_term.reshape(seq_len, -1)
    v_term = v_term.reshape(seq_len, -1)
    ctx_count = lax.axis_size("ctx")
    reach = min(ctx_count // 2 + 1, ctx_count - 1)

    def lower_slice(target):
        valid = (target >= 0).astype(jnp.float32)
        start = jnp.maximum(target, 0) * rows_here
        return (
            lax.dynamic_slice_in_dim(k_term, start, rows_here, 0) * valid,
            lax.dynamic_slice_in_dim(v_term, start, rows_here, 0) * valid,
        )

    def relay_step(step_count, carried):
        got_k, got_v = passed_along((carried[0], carried[1]), "ctx", -1)
        own_k, own_v = lower_slice(my_index - reach + step_count)
        return (got_k + own_k, got_v + own_v)

    k_owned, v_owned = lax.fori_loop(1, reach + 1, relay_step, lower_slice(my_index - reach))
    q_back, k_back, v_back = sent_together(
        (
            q_grad.astype(jnp.bfloat16).reshape(rows_here, -1),
            k_owned.astype(jnp.bfloat16),
            v_owned.astype(jnp.bfloat16),
        ),
        "dp",
        0,
        0,
        1,
    )
    return (attended, q_back[inverse], k_back[inverse], v_back[inverse])


def solution(mesh):
    placed = (
        P(("dp", "ctx"), None),
        P(("dp", "ctx"), None),
        P(("dp", "ctx"), None),
        P(("dp", "ctx"), None),
        P(("dp", "ctx")),
        P("dp", "ctx"),
    )
    return jax.shard_map(
        on_device,
        mesh=mesh,
        in_specs=placed,
        out_specs=(
            P(("dp", "ctx"), None),
            P(("dp", "ctx"), None),
            P(("dp", "ctx"), None),
            P(("dp", "ctx"), None),
        ),
        check_vma=False,
    )
```

profile of v0, /device:TPU:96, one launch (start us, length us, event | category | flops | bytes accessed | tf_op | source)
XLA Modules:
  0.0 770.2 jit_solution(12146616452097911510)
XLA Ops:
  13.0 31.0 %all_to_all.33 = bf16[4,32,9216]{2,1,0:T(8,128)(2,1)S(1)} all-to-all(bf16[4,32,9216]{2,1,0:T(8,128)(2,1)S(1)} %bitcast.154), channel_id=1, replica_groups=mesh['dp'=4,'ctx'=32] {'dp'}, dimensions={0} | all-to-all | bytes 4718592 | tf_op jit(solution)/shard_map/all_to_all | solution.py:22
  44.8 84.0 %all_gather.8 = s32[1,4096]{1,0:T(1,128)S(1)} all-gather(s32[1,128]{1,0:T(1,128)S(1)} %copy-done.10), channel_id=1, replica_groups=mesh['dp'=4,'ctx'=32] {'ctx'}, dimensions={1}, use_global_device_ids=true | all-gather | bytes 16896 | tf_op jit(solution)/shard_map/all_gather | solution.py:66
  134.2 15.4 %all-gather.2.cloned.1.call-done = bf16[4096,1024]{1,0:T(8,128)(2,1)} async-done(((bf16[128,1024]{1,0:T(8,128)(2,1)}), bf16[4096,1024]{1,0:T(8,128)(2,1)}) %all-gather.2.cloned.1.call-update) | async-done | bytes 8388624 | tf_op jit(solution)/shard_map/all_gather | solution.py:35
  161.7 35.8 %while.69 = (s32[]{:T(128)}, f32[4,8,128]{2,1,0:T(8,128)S(1)}, f32[4,8,128]{2,1,0:T(8,128)S(1)}, s32[]{:T(128)}, s32[4096]{0:T(1024)S(1)}, /*index=5*/s32[128]{0...) while((s32[]{:T(128)}, f32[4,8,128]{2,1,0:T(8,128)S(1)}, ...), condition=%wide.region_5.6_spmd.clone, body=%wide.region_0.5_spmd.clone.sunk | while | flops 553853568 | bytes 19825516 | solution.py:110
  204.2 51.2 %while.70 = (s32[]{:T(128)}, f32[128,4,8,128]{3,0,2,1:T(8,128)S(1)}, s32[]{:T(128)}, s32[4096]{0:T(1024)S(1)}, s32[128]{0:T(128)S(1)}, /*index=5*/s32[1,128]{1,0...) while((s32[]{:T(128)}, ...), condition=%wide.region_9.0_spmd.clone, body=%wide.region_6.9_spmd.clone.sunk | while | flops 1084949120 | bytes 8553309 | solution.py:136
  208.3 8.0 %conditional.10 = (f32[128,4,8,128]{3,0,2,1:T(8,128)S(1)}) conditional(s32[]{:T(128)} %convert_element_type.90, f32[128,4,8,128]{3,0,2,1:T(8,128)S(1)} %get-tuple-element.1734, (s32[512]{0:T(512)S(1)}, s32[1,128]{1,0:T(1,128)S(1)}, s32[]{:T(128)}, s32[512]{0:T(512)S(1)}, s32[]{:T(128)}, /*index=5*/bf16[4096,512]{0,1:T(8,128)(2,1)}, s32[]{:T(128)}, ...), branch_computations={%region_7.7_spmd, %region_8.8_spmd} | conditional | flops 1084949120 | bytes 8546324 | solution.py:134
  217.7 8.0 %conditional.10 = (f32[128,4,8,128]{3,0,2,1:T(8,128)S(1)}) conditional(s32[]{:T(128)} %convert_element_type.90, f32[128,4,8,128]{3,0,2,1:T(8,128)S(1)} %get-tuple-element.1734, (s32[512]{0:T(512)S(1)}, s32[1,128]{1,0:T(1,128)S(1)}, s32[]{:T(128)}, s32[512]{0:T(512)S(1)}, s32[]{:T(128)}, /*index=5*/bf16[4096,512]{0,1:T(8,128)(2,1)}, s32[]{:T(128)}, ...), branch_computations={%region_7.7_spmd, %region_8.8_spmd} | conditional | flops 1084949120 | bytes 8546324 | solution.py:134
  227.1 8.0 %conditional.10 = (f32[128,4,8,128]{3,0,2,1:T(8,128)S(1)}) conditional(s32[]{:T(128)} %convert_element_type.90, f32[128,4,8,128]{3,0,2,1:T(8,128)S(1)} %get-tuple-element.1734, (s32[512]{0:T(512)S(1)}, s32[1,128]{1,0:T(1,128)S(1)}, s32[]{:T(128)}, s32[512]{0:T(512)S(1)}, s32[]{:T(128)}, /*index=5*/bf16[4096,512]{0,1:T(8,128)(2,1)}, s32[]{:T(128)}, ...), branch_computations={%region_7.7_spmd, %region_8.8_spmd} | conditional | flops 1084949120 | bytes 8546324 | solution.py:134
  236.5 8.0 %conditional.10 = (f32[128,4,8,128]{3,0,2,1:T(8,128)S(1)}) conditional(s32[]{:T(128)} %convert_element_type.90, f32[128,4,8,128]{3,0,2,1:T(8,128)S(1)} %get-tuple-element.1734, (s32[512]{0:T(512)S(1)}, s32[1,128]{1,0:T(1,128)S(1)}, s32[]{:T(128)}, s32[512]{0:T(512)S(1)}, s32[]{:T(128)}, /*index=5*/bf16[4096,512]{0,1:T(8,128)(2,1)}, s32[]{:T(128)}, ...), branch_computations={%region_7.7_spmd, %region_8.8_spmd} | conditional | flops 1084949120 | bytes 8546324 | solution.py:134
  245.9 8.0 %conditional.10 = (f32[128,4,8,128]{3,0,2,1:T(8,128)S(1)}) conditional(s32[]{:T(128)} %convert_element_type.90, f32[128,4,8,128]{3,0,2,1:T(8,128)S(1)} %get-tuple-element.1734, (s32[512]{0:T(512)S(1)}, s32[1,128]{1,0:T(1,128)S(1)}, s32[]{:T(128)}, s32[512]{0:T(512)S(1)}, s32[]{:T(128)}, /*index=5*/bf16[4096,512]{0,1:T(8,128)(2,1)}, s32[]{:T(128)}, ...), branch_computations={%region_7.7_spmd, %region_8.8_spmd} | conditional | flops 1084949120 | bytes 8546324 | solution.py:134
  275.9 109.0 %while.71 = (s32[]{:T(128)}, f32[128,4,8,128]{3,0,2,1:T(8,128)S(1)}, f32[4096,4,128]{2,0,1:T(8,128)}, f32[4096,4,128]{2,0,1:T(8,128)}, s32[]{:T(128)}, /*index=5...) while((s32[]{:T(128)}, ...), condition=%wide.region_15.16_spmd.clone, body=%wide.region_12.15_spmd.clone.sunk | while | flops 2712338944 | bytes 106693712 | solution.py:187
  279.8 19.8 %conditional.11 = ((f32[128,4,8,128]{3,0,2,1:T(8,128)S(1)}, f32[4096,4,128]{2,0,1:T(8,128)}, f32[4096,4,128]{2,0,1:T(8,128)})) conditional(s32[]{:T(128)} %convert_element_type.91, (f32[128,4,8,128]{3,0,2,1:T(8,128)S(1)}, f32[4096,4,128]{2,0,1:T(8,128)}, f32[4096,4,128]{2,0,1:T(8,128)}) %tuple.187, (s32[512]{0:T(512)S(1)}, ...), branch_computations={%region_13.13_spmd, %region_14.14_spmd} | conditional | flops 2712338944 | bytes 106686640 | solution.py:184
  300.8 19.8 %conditional.11 = ((f32[128,4,8,128]{3,0,2,1:T(8,128)S(1)}, f32[4096,4,128]{2,0,1:T(8,128)}, f32[4096,4,128]{2,0,1:T(8,128)})) conditional(s32[]{:T(128)} %convert_element_type.91, (f32[128,4,8,128]{3,0,2,1:T(8,128)S(1)}, f32[4096,4,128]{2,0,1:T(8,128)}, f32[4096,4,128]{2,0,1:T(8,128)}) %tuple.187, (s32[512]{0:T(512)S(1)}, ...), branch_computations={%region_13.13_spmd, %region_14.14_spmd} | conditional | flops 2712338944 | bytes 106686640 | solution.py:184
  321.8 19.8 %conditional.11 = ((f32[128,4,8,128]{3,0,2,1:T(8,128)S(1)}, f32[4096,4,128]{2,0,1:T(8,128)}, f32[4096,4,128]{2,0,1:T(8,128)})) conditional(s32[]{:T(128)} %convert_element_type.91, (f32[128,4,8,128]{3,0,2,1:T(8,128)S(1)}, f32[4096,4,128]{2,0,1:T(8,128)}, f32[4096,4,128]{2,0,1:T(8,128)}) %tuple.187, (s32[512]{0:T(512)S(1)}, ...), branch_computations={%region_13.13_spmd, %region_14.14_spmd} | conditional | flops 2712338944 | bytes 106686640 | solution.py:184
  342.8 19.8 %conditional.11 = ((f32[128,4,8,128]{3,0,2,1:T(8,128)S(1)}, f32[4096,4,128]{2,0,1:T(8,128)}, f32[4096,4,128]{2,0,1:T(8,128)})) conditional(s32[]{:T(128)} %convert_element_type.91, (f32[128,4,8,128]{3,0,2,1:T(8,128)S(1)}, f32[4096,4,128]{2,0,1:T(8,128)}, f32[4096,4,128]{2,0,1:T(8,128)}) %tuple.187, (s32[512]{0:T(512)S(1)}, ...), branch_computations={%region_13.13_spmd, %region_14.14_spmd} | conditional | flops 2712338944 | bytes 106686640 | solution.py:184
  363.9 19.8 %conditional.11 = ((f32[128,4,8,128]{3,0,2,1:T(8,128)S(1)}, f32[4096,4,128]{2,0,1:T(8,128)}, f32[4096,4,128]{2,0,1:T(8,128)})) conditional(s32[]{:T(128)} %convert_element_type.91, (f32[128,4,8,128]{3,0,2,1:T(8,128)S(1)}, f32[4096,4,128]{2,0,1:T(8,128)}, f32[4096,4,128]{2,0,1:T(8,128)}) %tuple.187, (s32[512]{0:T(512)S(1)}, ...), branch_computations={%region_13.13_spmd, %region_14.14_spmd} | conditional | flops 2712338944 | bytes 106686640 | solution.py:184
  384.9 9.0 %copy.82 = f32[4096,4,128]{0,2,1:T(8,128)} copy(f32[4096,4,128]{2,0,1:T(8,128)} %get-tuple-element.1061) | data formatting | bytes 16777216 | tf_op jit(solution)/shard_map/while | solution.py:187
  393.9 8.9 %copy.81 = f32[4096,4,128]{0,2,1:T(8,128)} copy(f32[4096,4,128]{2,0,1:T(8,128)} %get-tuple-element.1060) | data formatting | bytes 16777216 | tf_op jit(solution)/shard_map/while | solution.py:187
  405.6 325.1 %while.68 = (s32[]{:T(128)}, f32[128,512]{1,0:T(8,128)}, f32[128,512]{1,0:T(8,128)}, s32[]{:T(128)}, f32[4096,512]{0,1:T(8,128)}, /*index=5*/f32[4096,512]{0,1:T(8,128)}, s32[]{:T(128)}, s32[]{:T(128)}, s32[]{:T(128)}, s32[]{:T(128)}) while((s32[]{:T(128)}, f32[128,512]{1,0:T(8,128)}, f32[128,512]{1,0:T(8,128)}, s32[]{:T(128)}, ...), condition=%wide.region_17.18_spmd, body=%wide.region_16.17_spmd.sunk | while | flops 262154 | bytes 5767445 | solution.py:211
  410.8 7.6 collective-permute-done
  441.6 8.5 %collective-permute-start = (f32[128,512]{1,0:T(8,128)}, f32[128,512]{1,0:T(8,128)S(1)}, u32[]{:S(2)}, u32[]{:S(2)}) collective-permute-start(f32[128,512]{1,0:T(8,128)} %get-tuple-element.1831), channel_id=1, source_target_pairs={{1,0},{2,1},{3,2},{4,3},{5,4},{6,5},{7,6},{8,7},{9,8},{10,9},{11,1... | collective-permute-start | bytes 786440 | tf_op jit(solution)/shard_map/while/body/eval_jaxpr/ppermute | solution.py:41
  461.3 8.8 %collective-permute-start = (f32[128,512]{1,0:T(8,128)}, f32[128,512]{1,0:T(8,128)S(1)}, u32[]{:S(2)}, u32[]{:S(2)}) collective-permute-start(f32[128,512]{1,0:T(8,128)} %get-tuple-element.1831), channel_id=1, source_target_pairs={{1,0},{2,1},{3,2},{4,3},{5,4},{6,5},{7,6},{8,7},{9,8},{10,9},{11,1... | collective-permute-start | bytes 786440 | tf_op jit(solution)/shard_map/while/body/eval_jaxpr/ppermute | solution.py:41
  473.4 15.9 %collective-permute-done = f32[128,512]{1,0:T(8,128)S(1)} collective-permute-done((f32[128,512]{1,0:T(8,128)}, f32[128,512]{1,0:T(8,128)S(1)}, u32[]{:S(2)}, u32[]{:S(2)}) %collective-permute-start) | collective-permute-done | bytes 262176 | tf_op jit(solution)/shard_map/while/body/eval_jaxpr/ppermute | solution.py:41
  498.1 9.3 %collective-permute-done = f32[128,512]{1,0:T(8,128)S(1)} collective-permute-done((f32[128,512]{1,0:T(8,128)}, f32[128,512]{1,0:T(8,128)S(1)}, u32[]{:S(2)}, u32[]{:S(2)}) %collective-permute-start) | collective-permute-done | bytes 262176 | tf_op jit(solution)/shard_map/while/body/eval_jaxpr/ppermute | solution.py:41
  518.8 9.6 %collective-permute-done = f32[128,512]{1,0:T(8,128)S(1)} collective-permute-done((f32[128,512]{1,0:T(8,128)}, f32[128,512]{1,0:T(8,128)S(1)}, u32[]{:S(2)}, u32[]{:S(2)}) %collective-permute-start) | collective-permute-done | bytes 262176 | tf_op jit(solution)/shard_map/while/body/eval_jaxpr/ppermute | solution.py:41
  550.2 8.5 %collective-permute-start = (f32[128,512]{1,0:T(8,128)}, f32[128,512]{1,0:T(8,128)S(1)}, u32[]{:S(2)}, u32[]{:S(2)}) collective-permute-start(f32[128,512]{1,0:T(8,128)} %get-tuple-element.1831), channel_id=1, source_target_pairs={{1,0},{2,1},{3,2},{4,3},{5,4},{6,5},{7,6},{8,7},{9,8},{10,9},{11,1... | collective-permute-start | bytes 786440 | tf_op jit(solution)/shard_map/while/body/eval_jaxpr/ppermute | solution.py:41
  570.6 8.8 %collective-permute-start = (f32[128,512]{1,0:T(8,128)}, f32[128,512]{1,0:T(8,128)S(1)}, u32[]{:S(2)}, u32[]{:S(2)}) collective-permute-start(f32[128,512]{1,0:T(8,128)} %get-tuple-element.1831), channel_id=1, source_target_pairs={{1,0},{2,1},{3,2},{4,3},{5,4},{6,5},{7,6},{8,7},{9,8},{10,9},{11,1... | collective-permute-start | bytes 786440 | tf_op jit(solution)/shard_map/while/body/eval_jaxpr/ppermute | solution.py:41
  590.5 8.8 %collective-permute-start = (f32[128,512]{1,0:T(8,128)}, f32[128,512]{1,0:T(8,128)S(1)}, u32[]{:S(2)}, u32[]{:S(2)}) collective-permute-start(f32[128,512]{1,0:T(8,128)} %get-tuple-element.1831), channel_id=1, source_target_pairs={{1,0},{2,1},{3,2},{4,3},{5,4},{6,5},{7,6},{8,7},{9,8},{10,9},{11,1... | collective-permute-start | bytes 786440 | tf_op jit(solution)/shard_map/while/body/eval_jaxpr/ppermute | solution.py:41
  610.0 8.3 %collective-permute-start = (f32[128,512]{1,0:T(8,128)}, f32[128,512]{1,0:T(8,128)S(1)}, u32[]{:S(2)}, u32[]{:S(2)}) collective-permute-start(f32[128,512]{1,0:T(8,128)} %get-tuple-element.1831), channel_id=1, source_target_pairs={{1,0},{2,1},{3,2},{4,3},{5,4},{6,5},{7,6},{8,7},{9,8},{10,9},{11,1... | collective-permute-start | bytes 786440 | tf_op jit(solution)/shard_map/while/body/eval_jaxpr/ppermute | solution.py:41
  629.1 7.5 collective-permute-start
  647.3 6.6 collective-permute-start
  744.6 11.4 %all-to-all-done.2 = bf16[4,32,5120]{2,1,0:T(8,128)(2,1)S(1)} async-done(((bf16[4,32,5120]{2,1,0:T(8,128)(2,1)}), bf16[4,32,5120]{2,1,0:T(8,128)(2,1)S(1)}, u32[]{:S(2)}, u32[]{:S(2)}) %all-to-all-start.2) | async-done | bytes 1310752 | tf_op jit(solution)/shard_map/all_to_all | solution.py:22
  (466 shorter events, 494.8 us)
Async XLA Ops:
  7.2 142.4 %all-gather.2.cloned.1.call-start = ((), (), s32[]{:S(2)}) async-start(), calls=%async_computation.3 | async-start | bytes 8650752 | tf_op jit(solution)/shard_map/all_gather | solution.py:35
  261.5 473.8 %all-to-all-start.1 = ((bf16[4,32,4096]{2,1,0:T(8,128)(2,1)}), bf16[4,32,4096]{2,1,0:T(8,128)(2,1)}, u32[]{:S(2)}, u32[]{:S(2)}) async-start(bf16[4,32,4096]{2,1,0:T(8,128)(2,1)} %all_to_all.25), calls=%async_computation.1 | async-start | bytes 2097152 | tf_op jit(solution)/shard_map/all_to_all | solution.py:139
  405.6 12.8 %collective-permute-start = (f32[128,512]{1,0:T(8,128)}, f32[128,512]{1,0:T(8,128)S(1)}, u32[]{:S(2)}, u32[]{:S(2)}) collective-permute-start(f32[128,512]{1,0:T(8,128)} %get-tuple-element.1831), channel_id=1, source_target_pairs={{1,0},{2,1},{3,2},{4,3},{5,4},{6,5},{7,6},{8,7},{9,8},{10,9},{11,1... | collective-permute-start | bytes 786440 | tf_op jit(solution)/shard_map/while/body/eval_jaxpr/ppermute | solution.py:41
  407.5 15.7 %collective-permute-start.1 = (f32[128,512]{1,0:T(8,128)}, f32[128,512]{1,0:T(8,128)S(1)}, u32[]{:S(2)}, u32[]{:S(2)}) collective-permute-start(f32[128,512]{1,0:T(8,128)} %get-tuple-element.1832), channel_id=1, source_target_pairs={{1,0},{2,1},{3,2},{4,3},{5,4},{6,5},{7,6},{8,7},{9,8},{10,9},{11,1... | collective-permute-start | bytes 786440 | tf_op jit(solution)/shard_map/while/body/eval_jaxpr/ppermute | solution.py:41
  424.0 12.2 %collective-permute-start = (f32[128,512]{1,0:T(8,128)}, f32[128,512]{1,0:T(8,128)S(1)}, u32[]{:S(2)}, u32[]{:S(2)}) collective-permute-start(f32[128,512]{1,0:T(8,128)} %get-tuple-element.1831), channel_id=1, source_target_pairs={{1,0},{2,1},{3,2},{4,3},{5,4},{6,5},{7,6},{8,7},{9,8},{10,9},{11,1... | collective-permute-start | bytes 786440 | tf_op jit(solution)/shard_map/while/body/eval_jaxpr/ppermute | solution.py:41
  429.2 11.6 %collective-permute-start.1 = (f32[128,512]{1,0:T(8,128)}, f32[128,512]{1,0:T(8,128)S(1)}, u32[]{:S(2)}, u32[]{:S(2)}) collective-permute-start(f32[128,512]{1,0:T(8,128)} %get-tuple-element.1832), channel_id=1, source_target_pairs={{1,0},{2,1},{3,2},{4,3},{5,4},{6,5},{7,6},{8,7},{9,8},{10,9},{11,1... | collective-permute-start | bytes 786440 | tf_op jit(solution)/shard_map/while/body/eval_jaxpr/ppermute | solution.py:41
  441.6 15.5 %collective-permute-start = (f32[128,512]{1,0:T(8,128)}, f32[128,512]{1,0:T(8,128)S(1)}, u32[]{:S(2)}, u32[]{:S(2)}) collective-permute-start(f32[128,512]{1,0:T(8,128)} %get-tuple-element.1831), channel_id=1, source_target_pairs={{1,0},{2,1},{3,2},{4,3},{5,4},{6,5},{7,6},{8,7},{9,8},{10,9},{11,1... | collective-permute-start | bytes 786440 | tf_op jit(solution)/shard_map/while/body/eval_jaxpr/ppermute | solution.py:41
  450.1 10.4 %collective-permute-start.1 = (f32[128,512]{1,0:T(8,128)}, f32[128,512]{1,0:T(8,128)S(1)}, u32[]{:S(2)}, u32[]{:S(2)}) collective-permute-start(f32[128,512]{1,0:T(8,128)} %get-tuple-element.1832), channel_id=1, source_target_pairs={{1,0},{2,1},{3,2},{4,3},{5,4},{6,5},{7,6},{8,7},{9,8},{10,9},{11,1... | collective-permute-start | bytes 786440 | tf_op jit(solution)/shard_map/while/body/eval_jaxpr/ppermute | solution.py:41
  461.3 28.0 %collective-permute-start = (f32[128,512]{1,0:T(8,128)}, f32[128,512]{1,0:T(8,128)S(1)}, u32[]{:S(2)}, u32[]{:S(2)}) collective-permute-start(f32[128,512]{1,0:T(8,128)} %get-tuple-element.1831), channel_id=1, source_target_pairs={{1,0},{2,1},{3,2},{4,3},{5,4},{6,5},{7,6},{8,7},{9,8},{10,9},{11,1... | collective-permute-start | bytes 786440 | tf_op jit(solution)/shard_map/while/body/eval_jaxpr/ppermute | solution.py:41
  470.1 22.0 %collective-permute-start.1 = (f32[128,512]{1,0:T(8,128)}, f32[128,512]{1,0:T(8,128)S(1)}, u32[]{:S(2)}, u32[]{:S(2)}) collective-permute-start(f32[128,512]{1,0:T(8,128)} %get-tuple-element.1832), channel_id=1, source_target_pairs={{1,0},{2,1},{3,2},{4,3},{5,4},{6,5},{7,6},{8,7},{9,8},{10,9},{11,1... | collective-permute-start | bytes 786440 | tf_op jit(solution)/shard_map/while/body/eval_jaxpr/ppermute | solution.py:41
  492.9 14.5 %collective-permute-start = (f32[128,512]{1,0:T(8,128)}, f32[128,512]{1,0:T(8,128)S(1)}, u32[]{:S(2)}, u32[]{:S(2)}) collective-permute-start(f32[128,512]{1,0:T(8,128)} %get-tuple-element.1831), channel_id=1, source_target_pairs={{1,0},{2,1},{3,2},{4,3},{5,4},{6,5},{7,6},{8,7},{9,8},{10,9},{11,1... | collective-permute-start | bytes 786440 | tf_op jit(solution)/shard_map/while/body/eval_jaxpr/ppermute | solution.py:41
  494.8 18.0 %collective-permute-start.1 = (f32[128,512]{1,0:T(8,128)}, f32[128,512]{1,0:T(8,128)S(1)}, u32[]{:S(2)}, u32[]{:S(2)}) collective-permute-start(f32[128,512]{1,0:T(8,128)} %get-tuple-element.1832), channel_id=1, source_target_pairs={{1,0},{2,1},{3,2},{4,3},{5,4},{6,5},{7,6},{8,7},{9,8},{10,9},{11,1... | collective-permute-start | bytes 786440 | tf_op jit(solution)/shard_map/while/body/eval_jaxpr/ppermute | solution.py:41
  513.6 14.9 %collective-permute-start = (f32[128,512]{1,0:T(8,128)}, f32[128,512]{1,0:T(8,128)S(1)}, u32[]{:S(2)}, u32[]{:S(2)}) collective-permute-start(f32[128,512]{1,0:T(8,128)} %get-tuple-element.1831), channel_id=1, source_target_pairs={{1,0},{2,1},{3,2},{4,3},{5,4},{6,5},{7,6},{8,7},{9,8},{10,9},{11,1... | collective-permute-start | bytes 786440 | tf_op jit(solution)/shard_map/while/body/eval_jaxpr/ppermute | solution.py:41
  515.5 15.8 %collective-permute-start.1 = (f32[128,512]{1,0:T(8,128)}, f32[128,512]{1,0:T(8,128)S(1)}, u32[]{:S(2)}, u32[]{:S(2)}) collective-permute-start(f32[128,512]{1,0:T(8,128)} %get-tuple-element.1832), channel_id=1, source_target_pairs={{1,0},{2,1},{3,2},{4,3},{5,4},{6,5},{7,6},{8,7},{9,8},{10,9},{11,1... | collective-permute-start | bytes 786440 | tf_op jit(solution)/shard_map/while/body/eval_jaxpr/ppermute | solution.py:41
  532.1 12.1 %collective-permute-start = (f32[128,512]{1,0:T(8,128)}, f32[128,512]{1,0:T(8,128)S(1)}, u32[]{:S(2)}, u32[]{:S(2)}) collective-permute-start(f32[128,512]{1,0:T(8,128)} %get-tuple-element.1831), channel_id=1, source_target_pairs={{1,0},{2,1},{3,2},{4,3},{5,4},{6,5},{7,6},{8,7},{9,8},{10,9},{11,1... | collective-permute-start | bytes 786440 | tf_op jit(solution)/shard_map/while/body/eval_jaxpr/ppermute | solution.py:41
  537.0 12.4 %collective-permute-start.1 = (f32[128,512]{1,0:T(8,128)}, f32[128,512]{1,0:T(8,128)S(1)}, u32[]{:S(2)}, u32[]{:S(2)}) collective-permute-start(f32[128,512]{1,0:T(8,128)} %get-tuple-element.1832), channel_id=1, source_target_pairs={{1,0},{2,1},{3,2},{4,3},{5,4},{6,5},{7,6},{8,7},{9,8},{10,9},{11,1... | collective-permute-start | bytes 786440 | tf_op jit(solution)/shard_map/while/body/eval_jaxpr/ppermute | solution.py:41
  550.2 15.5 %collective-permute-start = (f32[128,512]{1,0:T(8,128)}, f32[128,512]{1,0:T(8,128)S(1)}, u32[]{:S(2)}, u32[]{:S(2)}) collective-permute-start(f32[128,512]{1,0:T(8,128)} %get-tuple-element.1831), channel_id=1, source_target_pairs={{1,0},{2,1},{3,2},{4,3},{5,4},{6,5},{7,6},{8,7},{9,8},{10,9},{11,1... | collective-permute-start | bytes 786440 | tf_op jit(solution)/shard_map/while/body/eval_jaxpr/ppermute | solution.py:41
  558.6 11.2 %collective-permute-start.1 = (f32[128,512]{1,0:T(8,128)}, f32[128,512]{1,0:T(8,128)S(1)}, u32[]{:S(2)}, u32[]{:S(2)}) collective-permute-start(f32[128,512]{1,0:T(8,128)} %get-tuple-element.1832), channel_id=1, source_target_pairs={{1,0},{2,1},{3,2},{4,3},{5,4},{6,5},{7,6},{8,7},{9,8},{10,9},{11,1... | collective-permute-start | bytes 786440 | tf_op jit(solution)/shard_map/while/body/eval_jaxpr/ppermute | solution.py:41
  570.6 15.8 %collective-permute-start = (f32[128,512]{1,0:T(8,128)}, f32[128,512]{1,0:T(8,128)S(1)}, u32[]{:S(2)}, u32[]{:S(2)}) collective-permute-start(f32[128,512]{1,0:T(8,128)} %get-tuple-element.1831), channel_id=1, source_target_pairs={{1,0},{2,1},{3,2},{4,3},{5,4},{6,5},{7,6},{8,7},{9,8},{10,9},{11,1... | collective-permute-start | bytes 786440 | tf_op jit(solution)/shard_map/while/body/eval_jaxpr/ppermute | solution.py:41
  579.4 10.4 %collective-permute-start.1 = (f32[128,512]{1,0:T(8,128)}, f32[128,512]{1,0:T(8,128)S(1)}, u32[]{:S(2)}, u32[]{:S(2)}) collective-permute-start(f32[128,512]{1,0:T(8,128)} %get-tuple-element.1832), channel_id=1, source_target_pairs={{1,0},{2,1},{3,2},{4,3},{5,4},{6,5},{7,6},{8,7},{9,8},{10,9},{11,1... | collective-permute-start | bytes 786440 | tf_op jit(solution)/shard_map/while/body/eval_jaxpr/ppermute | solution.py:41
  590.5 15.5 %collective-permute-start = (f32[128,512]{1,0:T(8,128)}, f32[128,512]{1,0:T(8,128)S(1)}, u32[]{:S(2)}, u32[]{:S(2)}) collective-permute-start(f32[128,512]{1,0:T(8,128)} %get-tuple-element.1831), channel_id=1, source_target_pairs={{1,0},{2,1},{3,2},{4,3},{5,4},{6,5},{7,6},{8,7},{9,8},{10,9},{11,1... | collective-permute-start | bytes 786440 | tf_op jit(solution)/shard_map/while/body/eval_jaxpr/ppermute | solution.py:41
  599.3 10.0 %collective-permute-start.1 = (f32[128,512]{1,0:T(8,128)}, f32[128,512]{1,0:T(8,128)S(1)}, u32[]{:S(2)}, u32[]{:S(2)}) collective-permute-start(f32[128,512]{1,0:T(8,128)} %get-tuple-element.1832), channel_id=1, source_target_pairs={{1,0},{2,1},{3,2},{4,3},{5,4},{6,5},{7,6},{8,7},{9,8},{10,9},{11,1... | collective-permute-start | bytes 786440 | tf_op jit(solution)/shard_map/while/body/eval_jaxpr/ppermute | solution.py:41
  610.0 14.2 %collective-permute-start = (f32[128,512]{1,0:T(8,128)}, f32[128,512]{1,0:T(8,128)S(1)}, u32[]{:S(2)}, u32[]{:S(2)}) collective-permute-start(f32[128,512]{1,0:T(8,128)} %get-tuple-element.1831), channel_id=1, source_target_pairs={{1,0},{2,1},{3,2},{4,3},{5,4},{6,5},{7,6},{8,7},{9,8},{10,9},{11,1... | collective-permute-start | bytes 786440 | tf_op jit(solution)/shard_map/while/body/eval_jaxpr/ppermute | solution.py:41
  618.3 10.0 %collective-permute-start.1 = (f32[128,512]{1,0:T(8,128)}, f32[128,512]{1,0:T(8,128)S(1)}, u32[]{:S(2)}, u32[]{:S(2)}) collective-permute-start(f32[128,512]{1,0:T(8,128)} %get-tuple-element.1832), channel_id=1, source_target_pairs={{1,0},{2,1},{3,2},{4,3},{5,4},{6,5},{7,6},{8,7},{9,8},{10,9},{11,1... | collective-permute-start | bytes 786440 | tf_op jit(solution)/shard_map/while/body/eval_jaxpr/ppermute | solution.py:41
  629.1 12.4 %collective-permute-start = (f32[128,512]{1,0:T(8,128)}, f32[128,512]{1,0:T(8,128)S(1)}, u32[]{:S(2)}, u32[]{:S(2)}) collective-permute-start(f32[128,512]{1,0:T(8,128)} %get-tuple-element.1831), channel_id=1, source_target_pairs={{1,0},{2,1},{3,2},{4,3},{5,4},{6,5},{7,6},{8,7},{9,8},{10,9},{11,1... | collective-permute-start | bytes 786440 | tf_op jit(solution)/shard_map/while/body/eval_jaxpr/ppermute | solution.py:41
  636.5 10.0 %collective-permute-start.1 = (f32[128,512]{1,0:T(8,128)}, f32[128,512]{1,0:T(8,128)S(1)}, u32[]{:S(2)}, u32[]{:S(2)}) collective-permute-start(f32[128,512]{1,0:T(8,128)} %get-tuple-element.1832), channel_id=1, source_target_pairs={{1,0},{2,1},{3,2},{4,3},{5,4},{6,5},{7,6},{8,7},{9,8},{10,9},{11,1... | collective-permute-start | bytes 786440 | tf_op jit(solution)/shard_map/while/body/eval_jaxpr/ppermute | solution.py:41
  647.3 12.1 %collective-permute-start = (f32[128,512]{1,0:T(8,128)}, f32[128,512]{1,0:T(8,128)S(1)}, u32[]{:S(2)}, u32[]{:S(2)}) collective-permute-start(f32[128,512]{1,0:T(8,128)} %get-tuple-element.1831), channel_id=1, source_target_pairs={{1,0},{2,1},{3,2},{4,3},{5,4},{6,5},{7,6},{8,7},{9,8},{10,9},{11,1... | collective-permute-start | bytes 786440 | tf_op jit(solution)/shard_map/while/body/eval_jaxpr/ppermute | solution.py:41
  664.6 11.5 %collective-permute-start = (f32[128,512]{1,0:T(8,128)}, f32[128,512]{1,0:T(8,128)S(1)}, u32[]{:S(2)}, u32[]{:S(2)}) collective-permute-start(f32[128,512]{1,0:T(8,128)} %get-tuple-element.1831), channel_id=1, source_target_pairs={{1,0},{2,1},{3,2},{4,3},{5,4},{6,5},{7,6},{8,7},{9,8},{10,9},{11,1... | collective-permute-start | bytes 786440 | tf_op jit(solution)/shard_map/while/body/eval_jaxpr/ppermute | solution.py:41
  681.1 10.3 %collective-permute-start = (f32[128,512]{1,0:T(8,128)}, f32[128,512]{1,0:T(8,128)S(1)}, u32[]{:S(2)}, u32[]{:S(2)}) collective-permute-start(f32[128,512]{1,0:T(8,128)} %get-tuple-element.1831), channel_id=1, source_target_pairs={{1,0},{2,1},{3,2},{4,3},{5,4},{6,5},{7,6},{8,7},{9,8},{10,9},{11,1... | collective-permute-start | bytes 786440 | tf_op jit(solution)/shard_map/while/body/eval_jaxpr/ppermute | solution.py:41
  686.9 10.2 %collective-permute-start.1 = (f32[128,512]{1,0:T(8,128)}, f32[128,512]{1,0:T(8,128)S(1)}, u32[]{:S(2)}, u32[]{:S(2)}) collective-permute-start(f32[128,512]{1,0:T(8,128)} %get-tuple-element.1832), channel_id=1, source_target_pairs={{1,0},{2,1},{3,2},{4,3},{5,4},{6,5},{7,6},{8,7},{9,8},{10,9},{11,1... | collective-permute-start | bytes 786440 | tf_op jit(solution)/shard_map/while/body/eval_jaxpr/ppermute | solution.py:41
  714.2 10.0 %collective-permute-start = (f32[128,512]{1,0:T(8,128)}, f32[128,512]{1,0:T(8,128)S(1)}, u32[]{:S(2)}, u32[]{:S(2)}) collective-permute-start(f32[128,512]{1,0:T(8,128)} %get-tuple-element.1831), channel_id=1, source_target_pairs={{1,0},{2,1},{3,2},{4,3},{5,4},{6,5},{7,6},{8,7},{9,8},{10,9},{11,1... | collective-permute-start | bytes 786440 | tf_op jit(solution)/shard_map/while/body/eval_jaxpr/ppermute | solution.py:41
  735.3 20.8 %all-to-all-start.2 = ((bf16[4,32,5120]{2,1,0:T(8,128)(2,1)}), bf16[4,32,5120]{2,1,0:T(8,128)(2,1)S(1)}, u32[]{:S(2)}, u32[]{:S(2)}) async-start(bf16[4,32,5120]{2,1,0:T(8,128)(2,1)} %pad_maximum_fusion.1), calls=%async_computation.2 | async-start | bytes 2621440 | tf_op jit(solution)/shard_map/all_to_all | solution.py:22
  (29 other events, 188.6 us)
Sparse Core Ops, SparseCore 0:
  44.9 104.6 all-gather.1
where the time goes:
time: 768 us; the launch traced here: 770 us
  waiting for transfers between devices  166 us (22%)
  starting transfers between devices  145 us (19%)
  local copies, waits for them, and re-layouts  139 us (18%)
  matrix products  125 us (16%)
  blocking collectives  115 us (15%)
  other arithmetic  47.8 us (6%)
  loops' own time  18.1 us (2%)
  between operations  14.3 us (2%)
    ppermute x34, waiting for transfers between devices, passed_along(): lax.ppermute(value, axis, [(source, source + steps) for source in range(f...  139 us
    ppermute x34, starting transfers between devices, passed_along(): lax.ppermute(value, axis, [(source, source + steps) for source in range(f...  137 us
    all_gather x1, blocking collectives, on_device(): lax.all_gather(segments, 'ctx', axis=1, tiled=True)  84 us
    dot_general x5, matrix products, grad_compute(): jnp.einsum('kgqs,qkgd->skd', weights, d_heads, preferred_element_type=jnp...  31.8 us
    all_to_all x1, blocking collectives, sent_together(): lax.all_to_all(both, axis, split_axis=split_dim, concat_axis=concat_dim,...  31 us
    dot_general x5, matrix products, output_compute(): jnp.einsum('kgqs,skd->qkgd', weights, val_blk, preferred_element_type=jnp...  27.5 us
    add x34, other arithmetic, relay_step(): return (got_k + own_k, got_v + own_v)  25.3 us
    dot_general x5, matrix products, grad_compute(): jnp.einsum('kgqs,qkgd->skd', dscore, q_heads, preferred_element_type=jnp....  22.2 us
  transfers between devices with their start and end apart: 37, of which 36 were waited for; matrix products, arithmetic and copies ran while one was open for 26% of the time, Pallas kernels for 0%

commit v1 on v0

v1 whole, which is shorter than its diff:
```python
import functools

import jax
import jax.numpy as jnp
from jax import lax
from jax.experimental import pallas as pl
from jax.experimental.pallas import tpu as pltpu
from jax.sharding import PartitionSpec as P

HEADS = 32
KV_HEADS = 4
HEAD_DIM = 128
GROUPS = HEADS // KV_HEADS
DOCS = 6
NEG = -1e30
LOG2E = 1.4426950408889634
SHARE = 32
TOK = 128
SEQ = 4096
TQ = 256
TK = 512

IN_ROWS = 4 * SHARE + 8
OUT_ROWS = 4 * SHARE


def dot(a, b):
    return jnp.dot(a, b, preferred_element_type=jnp.float32)


def plan_matrix(plan_ref):
    rows = lax.broadcasted_iota(jnp.int32, (TOK, TOK), 0)
    return jnp.where(rows == plan_ref[...], 1.0, 0.0).astype(jnp.float32)


def pack_kernel(plan_ref, seg_ref, q_ref, d_ref, k_ref, v_ref, o_ref):
    pick = plan_matrix(plan_ref).T.astype(jnp.bfloat16)
    seg_rows = jnp.broadcast_to(seg_ref[...].astype(jnp.float32), (8, TOK)).astype(jnp.bfloat16)
    k_rows = dot(pick, k_ref[...]).astype(jnp.bfloat16)
    v_rows = dot(pick, v_ref[...]).astype(jnp.bfloat16)
    for pair in range(GROUPS // 2):
        at = slice(pair * 256, pair * 256 + 256)
        q_rows = dot(pick, q_ref[:, at]).astype(jnp.bfloat16)
        d_rows = dot(pick, d_ref[:, at]).astype(jnp.bfloat16)
        for core in range(2):
            cols = slice(core * HEAD_DIM, core * HEAD_DIM + HEAD_DIM)
            for b in range(4):
                rows = slice(b * SHARE, b * SHARE + SHARE)
                to = (b // 2, core, b % 2, pair)
                o_ref[to + (slice(0, 32),)] = q_rows[rows, cols]
                o_ref[to + (slice(32, 64),)] = d_rows[rows, cols]
                o_ref[to + (slice(64, 96),)] = k_rows[rows, :]
                o_ref[to + (slice(96, 128),)] = v_rows[rows, :]
                o_ref[to + (slice(128, 136),)] = seg_rows


def pack(queries, key_proj, value_proj, out_grad, row_plan, segments):
    wide = GROUPS * HEAD_DIM
    return pl.pallas_call(
        pack_kernel,
        grid=(KV_HEADS,),
        in_specs=[
            pl.BlockSpec((1, TOK), lambda g: (0, 0)),
            pl.BlockSpec((1, TOK), lambda g: (0, 0)),
            pl.BlockSpec((TOK, wide), lambda g: (0, g)),
            pl.BlockSpec((TOK, wide), lambda g: (0, g)),
            pl.BlockSpec((TOK, HEAD_DIM), lambda g: (0, g)),
            pl.BlockSpec((TOK, HEAD_DIM), lambda g: (0, g)),
        ],
        out_specs=pl.BlockSpec(
            (2, 2, 2, GROUPS // 2, IN_ROWS, HEAD_DIM), lambda g: (0, 0, 0, g, 0, 0)
        ),
        out_shape=jax.ShapeDtypeStruct((2, 2, 2, 16, IN_ROWS, HEAD_DIM), jnp.bfloat16),
        name="pack",
    )(row_plan.reshape(1, TOK), segments, queries, out_grad, key_proj, value_proj)


def unpack_kernel(plan_ref, y_ref, att_ref, qg_ref, kg_ref, vg_ref):
    put = plan_matrix(plan_ref).astype(jnp.bfloat16)

    def slots(core, pair, first):
        parts = [
            y_ref[b // 2, core, b % 2, pair, slice(first, first + SHARE)] for b in range(4)
        ]
        return jnp.concatenate(parts, axis=0)

    k_sum = jnp.zeros((TOK, HEAD_DIM), jnp.float32)
    v_sum = jnp.zeros((TOK, HEAD_DIM), jnp.float32)
    for pair in range(GROUPS // 2):
        for core in range(2):
            at = slice((pair * 2 + core) * HEAD_DIM, (pair * 2 + core + 1) * HEAD_DIM)
            att_ref[:, at] = dot(put, slots(core, pair, 0)).astype(jnp.bfloat16)
            qg_ref[:, at] = dot(put, slots(core, pair, 32)).astype(jnp.bfloat16)
            k_sum = k_sum + slots(core, pair, 64).astype(jnp.float32)
            v_sum = v_sum + slots(core, pair, 96).astype(jnp.float32)
    kg_ref[...] = dot(put, k_sum.astype(jnp.bfloat16)).astype(jnp.bfloat16)
    vg_ref[...] = dot(put, v_sum.astype(jnp.bfloat16)).astype(jnp.bfloat16)


def unpack(back, row_plan):
    wide = GROUPS * HEAD_DIM
    return pl.pallas_call(
        unpack_kernel,
        grid=(KV_HEADS,),
        in_specs=[
            pl.BlockSpec((1, TOK), lambda g: (0, 0)),
            pl.BlockSpec(
                (2, 2, 2, GROUPS // 2, OUT_ROWS, HEAD_DIM), lambda g: (0, 0, 0, g, 0, 0)
            ),
        ],
        out_specs=[
            pl.BlockSpec((TOK, wide), lambda g: (0, g)),
            pl.BlockSpec((TOK, wide), lambda g: (0, g)),
            pl.BlockSpec((TOK, HEAD_DIM), lambda g: (0, g)),
            pl.BlockSpec((TOK, HEAD_DIM), lambda g: (0, g)),
        ],
        out_shape=[
            jax.ShapeDtypeStruct((TOK, HEADS * HEAD_DIM), jnp.bfloat16),
            jax.ShapeDtypeStruct((TOK, HEADS * HEAD_DIM), jnp.bfloat16),
            jax.ShapeDtypeStruct((TOK, KV_HEADS * HEAD_DIM), jnp.bfloat16),
            jax.ShapeDtypeStruct((TOK, KV_HEADS * HEAD_DIM), jnp.bfloat16),
        ],
        name="unpack",
    )(row_plan.reshape(1, TOK), back)


def attention_kernel(
    group_ref, z_ref, o_ref, q_s, d_s, k_s, v_s, qt_s, dt_s, kt_s, vt_s, s_s, dk_s, dv_s, ot_s, qg_s
):
    scaling = HEAD_DIM ** (-0.5)
    to_exp2 = scaling * LOG2E

    def lay_out(c, carry):
        at = pl.ds(pl.multiple_of(c * TOK, TOK), TOK)
        for n, (rows_s, cols_s) in enumerate(((q_s, qt_s), (d_s, dt_s), (k_s, kt_s), (v_s, vt_s))):
            tile = z_ref[:, c, n * SHARE : n * SHARE + SHARE, :].reshape(TOK, HEAD_DIM)
            rows_s[at, :] = tile
            cols_s[:, at] = tile.T
        dk_s[at, :] = jnp.zeros((TOK, HEAD_DIM), jnp.float32)
        dv_s[at, :] = jnp.zeros((TOK, HEAD_DIM), jnp.float32)
        return carry

    lax.fori_loop(0, SEQ // TOK, lay_out, 0)

    ids = z_ref[group_ref[0], :, 4 * SHARE : 4 * SHARE + 8, :].astype(jnp.float32)
    cuts = [
        (jnp.sum((ids < float(doc)).astype(jnp.float32)) * 0.125).astype(jnp.int32)
        for doc in range(1, DOCS)
    ]

    def doc_start(position):
        start = jnp.zeros_like(position)
        for cut in cuts:
            start = jnp.maximum(start, jnp.where(position >= cut, cut, 0))
        return start

    def query_tile(i, carry):
        first_row = i * TQ
        q_at = pl.ds(pl.multiple_of(first_row, TQ), TQ)
        first_key = doc_start(first_row)
        lo = first_key // TK
        hi = (first_row + TQ - 1) // TK + 1
        rows = first_row + lax.broadcasted_iota(jnp.int32, (1, TQ), 1)
        starts = doc_start(rows)
        qt = qt_s[:, q_at]
        dt = dt_s[:, q_at]

        def score_step(j, top):
            k_at = pl.ds(pl.multiple_of(j * TK, TK), TK)
            scores = dot(k_s[k_at, :], qt)
            keys = j * TK + lax.broadcasted_iota(jnp.int32, (TK, TQ), 0)
            visible = (keys <= rows) & (keys >= starts)
            scores = jnp.where(visible, scores, NEG)
            s_s[k_at, :] = scores
            return jnp.maximum(top, jnp.max(scores.reshape(TK // 8, 8, TQ), axis=0))

        top = lax.fori_loop(lo, hi, score_step, jnp.full((8, TQ), NEG, jnp.float32))
        top = jnp.max(top, axis=0, keepdims=True)

        def exp_step(j, total):
            k_at = pl.ds(pl.multiple_of(j * TK, TK), TK)
            part = jnp.exp2((s_s[k_at, :] - top) * to_exp2)
            s_s[k_at, :] = part
            return total + jnp.sum(part.reshape(TK // 8, 8, TQ), axis=0)

        total = lax.fori_loop(lo, hi, exp_step, jnp.zeros((8, TQ), jnp.float32))
        share = 1.0 / jnp.sum(total, axis=0, keepdims=True)

        ot_s[...] = jnp.zeros_like(ot_s)
        qg_s[...] = jnp.zeros_like(qg_s)

        def out_step(j, carry):
            k_at = pl.ds(pl.multiple_of(j * TK, TK), TK)
            weights = (s_s[k_at, :] * share).astype(jnp.bfloat16)
            ot_s[...] += dot(vt_s[:, k_at], weights)
            return carry

        lax.fori_loop(lo, hi, out_step, 0)
        out_t = ot_s[...]
        row_dot = jnp.sum(dt.astype(jnp.float32) * out_t, axis=0, keepdims=True)

        def grad_step(j, carry):
            k_at = pl.ds(pl.multiple_of(j * TK, TK), TK)
            probs = s_s[k_at, :] * share
            dprobs = dot(v_s[k_at, :], dt)
            dscore = (probs * (dprobs - row_dot) * scaling).astype(jnp.bfloat16)
            dv_s[k_at, :] += dot(probs.astype(jnp.bfloat16), d_s[q_at, :])
            dk_s[k_at, :] += dot(dscore, q_s[q_at, :])
            qg_s[...] += dot(kt_s[:, k_at], dscore)
            return carry

        lax.fori_loop(lo, hi, grad_step, 0)

        out_rows = out_t.astype(jnp.bfloat16).T
        grad_rows = qg_s[...].astype(jnp.bfloat16).T
        for n in range(TQ // TOK):
            c = i * (TQ // TOK) + n
            at = slice(n * TOK, n * TOK + TOK)
            o_ref[:, c, 0:32, :] = out_rows[at].reshape(4, SHARE, HEAD_DIM)
            o_ref[:, c, 32:64, :] = grad_rows[at].reshape(4, SHARE, HEAD_DIM)
        return carry

    lax.fori_loop(0, SEQ // TQ, query_tile, 0)

    def give_back(c, carry):
        at = pl.ds(pl.multiple_of(c * TOK, TOK), TOK)
        o_ref[:, c, 64:96, :] = dk_s[at, :].astype(jnp.bfloat16).reshape(4, SHARE, HEAD_DIM)
        o_ref[:, c, 96:128, :] = dv_s[at, :].astype(jnp.bfloat16).reshape(4, SHARE, HEAD_DIM)
        return carry

    lax.fori_loop(0, SEQ // TOK, give_back, 0)


def attention(group, z):
    tall = pltpu.VMEM((SEQ, HEAD_DIM), jnp.bfloat16)
    flat = pltpu.VMEM((HEAD_DIM, SEQ), jnp.bfloat16)
    return pl.pallas_call(
        attention_kernel,
        in_specs=[
            pl.BlockSpec(memory_space=pltpu.SMEM),
            pl.BlockSpec(memory_space=pltpu.VMEM),
        ],
        out_specs=pl.BlockSpec(memory_space=pltpu.VMEM),
        out_shape=jax.ShapeDtypeStruct((4, 32, OUT_ROWS, HEAD_DIM), jnp.bfloat16),
        scratch_shapes=[tall] * 4
        + [flat] * 4
        + [
            pltpu.VMEM((SEQ, TQ), jnp.float32),
            pltpu.VMEM((SEQ, HEAD_DIM), jnp.float32),
            pltpu.VMEM((SEQ, HEAD_DIM), jnp.float32),
            pltpu.VMEM((HEAD_DIM, TQ), jnp.float32),
            pltpu.VMEM((HEAD_DIM, TQ), jnp.float32),
        ],
        compiler_params=pltpu.CompilerParams(vmem_limit_bytes=56 << 20),
        name="attention",
    )(group, z)


def on_device(queries, key_proj, value_proj, out_grad, row_plan, segments):
    sent = pack(queries, key_proj, value_proj, out_grad, row_plan, segments)
    here = lax.all_to_all(
        sent.reshape(TOK, IN_ROWS, HEAD_DIM), ("dp", "ctx"), split_axis=0, concat_axis=0, tiled=True
    )
    group = (lax.axis_index("dp") // 2) * 2 + lax.axis_index("ctx") // 16
    done = attention(
        group.astype(jnp.int32).reshape(1), here.reshape(4, 32, IN_ROWS, HEAD_DIM)
    )
    back = lax.all_to_all(
        done.reshape(TOK, OUT_ROWS, HEAD_DIM), ("dp", "ctx"), split_axis=0, concat_axis=0, tiled=True
    )
    return tuple(unpack(back.reshape(2, 2, 2, 16, OUT_ROWS, HEAD_DIM), row_plan))


def solution(mesh):
    rows = P(("dp", "ctx"), None)
    return jax.shard_map(
        on_device,
        mesh=mesh,
        in_specs=(rows, rows, rows, rows, P(("dp", "ctx")), P("dp", "ctx")),
        out_specs=(rows, rows, rows, rows),
        check_vma=False,
    )
```

time: 768 us -> 186 us (0.24)
  the two profiles are of different devices: /device:TPU:96 before, /device:TPU:1 now
where the time goes in v1:
time: 186 us; the launch traced here: 185 us
  blocking collectives  58.7 us (32%)
  waiting for transfers between devices  56.8 us (31%)
  Pallas kernels  56.6 us (30%)
  starting transfers between devices  11.9 us (6%)
    all_to_all x1, blocking collectives, on_device(): lax.all_to_all(done.reshape(TOK, OUT_ROWS, HEAD_DIM), ('dp', 'ctx'), spli...  58.7 us
    all_to_all x1, waiting for transfers between devices, on_device(): lax.all_to_all(sent.reshape(TOK, IN_ROWS, HEAD_DIM), ('dp', 'ctx'), split...  56.8 us
    pallas_call x1, Pallas kernels, attention(): pl.pallas_call(attention_kernel, in_specs=[pl.BlockSpec(memory_space=pltp...  46.9 us
    all_to_all x1, starting transfers between devices, on_device(): lax.all_to_all(sent.reshape(TOK, IN_ROWS, HEAD_DIM), ('dp', 'ctx'), split...  11.9 us
    pallas_call x1, Pallas kernels, pack(): pl.pallas_call(pack_kernel, grid=(KV_HEADS,), in_specs=[pl.BlockSpec((1,...  4.94 us
    pallas_call x1, Pallas kernels, unpack(): pl.pallas_call(unpack_kernel, grid=(KV_HEADS,), in_specs=[pl.BlockSpec((1...  4.76 us
  transfers between devices with their start and end apart: 1, of which 1 were waited for; matrix products, arithmetic and copies ran while one was open for 0% of the time, Pallas kernels for 0%

profile of v1, /device:TPU:1, one launch (start us, length us, event | category | flops | bytes accessed | tf_op | source)
XLA Modules:
  0.0 184.7 jit_solution(7269461668899453146)
XLA Ops:
  0.6 4.9 %pack.1 = bf16[2,2,2,16,136,128]{5,4,3,2,1,0:T(8,128)(2,1)} custom-call(s32[1,128]{1,0:T(1,128)} %bitcast.9, s32[1,128]{1,0:T(1,128)} %seg_ref.1, bf16[128,4096]{1,0:T(8,128)(2,1)} %q_ref.1, bf16[128,4096]{1,0:T(8,128)(2,1)} %d_ref.1, bf16[128,512]{1,0:T(8,128)(2,1)} %k_ref.1, bf16[128,512]{1,0:T(8,128)(2,1)} %v_ref.1), custom_call_target="tpu_custom_call" | custom-call | tf_op jit(solution)/shard_map/pack/pallas_call | solution.py:59
  5.6 11.9 %all-to-all-start = ((bf16[128,136,128]{2,1,0:T(8,128)(2,1)}), bf16[128,136,128]{2,1,0:T(8,128)(2,1)}, u32[]{:S(2)}, u32[]{:S(2)}) async-start(bf16[128,136,128]{2,1,0:T(8,128)(2,1)} %bitcast.6), calls=%async_computation | async-start | bytes 8912896 | tf_op jit(solution)/shard_map/all_to_all | solution.py:261
  17.5 56.8 %all-to-all-done = bf16[128,136,128]{2,1,0:T(8,128)(2,1)} async-done(((bf16[128,136,128]{2,1,0:T(8,128)(2,1)}), bf16[128,136,128]{2,1,0:T(8,128)(2,1)}, u32[]{:S(2)}, u32[]{:S(2)}) %all-to-all-start) | async-done | bytes 4456480 | tf_op jit(solution)/shard_map/all_to_all | solution.py:261
  74.3 46.9 %attention.1 = bf16[4,32,128,128]{3,2,1,0:T(8,128)(2,1)} custom-call(s32[1]{0:T(128)} %bitcast.1.group_ref, bf16[4,32,136,128]{3,2,1,0:T(8,128)(2,1)} %bitcast.3.z_ref), custom_call_target="tpu_custom_call" | custom-call | tf_op jit(solution)/shard_map/attention/pallas_call | solution.py:237
  121.2 58.7 %all_to_all.10 = bf16[128,128,128]{2,1,0:T(8,128)(2,1)} all-to-all(bf16[128,128,128]{2,1,0:T(8,128)(2,1)} %bitcast.8), channel_id=1, replica_groups=mesh['dp'=4,'ctx'=32] {'dp','ctx'}, dimensions={0} | all-to-all | bytes 8388608 | tf_op jit(solution)/shard_map/all_to_all | solution.py:268
  179.9 4.8 %unpack.1 = (bf16[128,4096]{1,0:T(8,128)(2,1)}, bf16[128,4096]{1,0:T(8,128)(2,1)}, bf16[128,512]{1,0:T(8,128)(2,1)}, bf16[128,512]{1,0:T(8,128)(2,1)}) custom-call(s32[1,128]{1,0:T(1,128)} %bitcast.10, bf16[2,2,2,16,128,128]{5,4,3,2,1,0:T(8,128)(2,1)} %bitcast.7), custom_call_target="tpu_custom_call" | custom-call | tf_op jit(solution)/shard_map/unpack/pallas_call | solution.py:102
Async XLA Ops:
  5.6 68.7 %all-to-all-start = ((bf16[128,136,128]{2,1,0:T(8,128)(2,1)}), bf16[128,136,128]{2,1,0:T(8,128)(2,1)}, u32[]{:S(2)}, u32[]{:S(2)}) async-start(bf16[128,136,128]{2,1,0:T(8,128)(2,1)} %bitcast.6), calls=%async_computation | async-start | bytes 8912896 | tf_op jit(solution)/shard_map/all_to_all | solution.py:261

commit v2 on v1

v2 whole, which is shorter than its diff:
```python
import functools

import jax
import jax.numpy as jnp
from jax import lax
from jax.experimental import pallas as pl
from jax.experimental.pallas import tpu as pltpu
from jax.sharding import PartitionSpec as P

HEADS = 32
KV_HEADS = 4
HEAD_DIM = 128
GROUPS = HEADS // KV_HEADS
DOCS = 6
NEG = -1e30
LOG2E = 1.4426950408889634
SHARE = 32
TOK = 128
SEQ = 4096
TQ = 256
TK = 512

IN_ROWS = 3 * SHARE + 8
OUT_ROWS = 3 * SHARE
PIECES = 4


def dot(a, b):
    return jnp.dot(a, b, preferred_element_type=jnp.float32)


def dot_nt(a, b):
    return lax.dot_general(a, b, (((1,), (1,)), ((), ())), preferred_element_type=jnp.float32)


def plan_matrix(plan_ref):
    rows = lax.broadcasted_iota(jnp.int32, (TOK, TOK), 0)
    return jnp.where(rows == plan_ref[...], 1.0, 0.0).astype(jnp.float32)


def pack_kernel(plan_ref, seg_ref, q_ref, d_ref, k_ref, v_ref, o_ref):
    pick = plan_matrix(plan_ref).T.astype(jnp.bfloat16)
    seg_rows = jnp.broadcast_to(seg_ref[...].astype(jnp.float32), (8, TOK)).astype(jnp.bfloat16)
    k_rows = dot(pick, k_ref[...]).astype(jnp.bfloat16)
    v_rows = dot(pick, v_ref[...]).astype(jnp.bfloat16)
    for pair in range(GROUPS // 2):
        at = slice(pair * 256, pair * 256 + 256)
        q_rows = dot(pick, q_ref[:, at]).astype(jnp.bfloat16)
        d_rows = dot(pick, d_ref[:, at]).astype(jnp.bfloat16)
        for core in range(2):
            cols = slice(core * HEAD_DIM, core * HEAD_DIM + HEAD_DIM)
            for b in range(4):
                rows = slice(b * SHARE, b * SHARE + SHARE)
                to = (b // 2, core, b % 2, pair)
                o_ref[to + (slice(0, 32),)] = q_rows[rows, cols]
                o_ref[to + (slice(32, 64),)] = d_rows[rows, cols]
                o_ref[to + (slice(64, 96),)] = (k_rows, v_rows)[core][rows, :]
                o_ref[to + (slice(96, 104),)] = seg_rows


def pack(queries, key_proj, value_proj, out_grad, row_plan, segments):
    wide = GROUPS * HEAD_DIM
    return pl.pallas_call(
        pack_kernel,
        grid=(KV_HEADS,),
        in_specs=[
            pl.BlockSpec((1, TOK), lambda g: (0, 0)),
            pl.BlockSpec((1, TOK), lambda g: (0, 0)),
            pl.BlockSpec((TOK, wide), lambda g: (0, g)),
            pl.BlockSpec((TOK, wide), lambda g: (0, g)),
            pl.BlockSpec((TOK, HEAD_DIM), lambda g: (0, g)),
            pl.BlockSpec((TOK, HEAD_DIM), lambda g: (0, g)),
        ],
        out_specs=pl.BlockSpec(
            (2, 2, 2, GROUPS // 2, IN_ROWS, HEAD_DIM), lambda g: (0, 0, 0, g, 0, 0)
        ),
        out_shape=jax.ShapeDtypeStruct((2, 2, 2, 16, IN_ROWS, HEAD_DIM), jnp.bfloat16),
        name="pack",
    )(row_plan.reshape(1, TOK), segments, queries, out_grad, key_proj, value_proj)


def unpack_kernel(plan_ref, y_ref, att_ref, qg_ref, kg_ref, vg_ref):
    put = plan_matrix(plan_ref).astype(jnp.bfloat16)

    def slots(core, pair, first):
        parts = [
            y_ref[b // 2, core, b % 2, pair, slice(first, first + SHARE)] for b in range(4)
        ]
        return jnp.concatenate(parts, axis=0)

    k_sum = jnp.zeros((TOK, HEAD_DIM), jnp.float32)
    v_sum = jnp.zeros((TOK, HEAD_DIM), jnp.float32)
    for pair in range(GROUPS // 2):
        for core in range(2):
            at = slice((pair * 2 + core) * HEAD_DIM, (pair * 2 + core + 1) * HEAD_DIM)
            att_ref[:, at] = dot(put, slots(core, pair, 0)).astype(jnp.bfloat16)
            qg_ref[:, at] = dot(put, slots(core, pair, 32)).astype(jnp.bfloat16)
        k_sum = k_sum + slots(0, pair, 64).astype(jnp.float32)
        v_sum = v_sum + slots(1, pair, 64).astype(jnp.float32)
    kg_ref[...] = dot(put, k_sum.astype(jnp.bfloat16)).astype(jnp.bfloat16)
    vg_ref[...] = dot(put, v_sum.astype(jnp.bfloat16)).astype(jnp.bfloat16)


def unpack(back, row_plan):
    wide = GROUPS * HEAD_DIM
    return pl.pallas_call(
        unpack_kernel,
        grid=(KV_HEADS,),
        in_specs=[
            pl.BlockSpec((1, TOK), lambda g: (0, 0)),
            pl.BlockSpec(
                (2, 2, 2, GROUPS // 2, OUT_ROWS, HEAD_DIM), lambda g: (0, 0, 0, g, 0, 0)
            ),
        ],
        out_specs=[
            pl.BlockSpec((TOK, wide), lambda g: (0, g)),
            pl.BlockSpec((TOK, wide), lambda g: (0, g)),
            pl.BlockSpec((TOK, HEAD_DIM), lambda g: (0, g)),
            pl.BlockSpec((TOK, HEAD_DIM), lambda g: (0, g)),
        ],
        out_shape=[
            jax.ShapeDtypeStruct((TOK, HEADS * HEAD_DIM), jnp.bfloat16),
            jax.ShapeDtypeStruct((TOK, HEADS * HEAD_DIM), jnp.bfloat16),
            jax.ShapeDtypeStruct((TOK, KV_HEADS * HEAD_DIM), jnp.bfloat16),
            jax.ShapeDtypeStruct((TOK, KV_HEADS * HEAD_DIM), jnp.bfloat16),
        ],
        name="unpack",
    )(row_plan.reshape(1, TOK), back)


def attention_kernel(
    z_ref,
    other_ref,
    o_ref,
    keep_ref,
    give_ref,
    qd_b,
    kv_b,
    seg_b,
    o_b,
    q_s,
    qa_s,
    d_s,
    k_s,
    ka_s,
    v_s,
    dt_s,
    kt_s,
    vt_s,
    p_even,
    p_odd,
    tops_even,
    tops_odd,
    rows_even,
    rows_odd,
    dk_s,
    dv_s,
    ot_s,
    qg_s,
    top_s,
    sum_s,
    in_sem,
    seg_sem,
    out_sem,
    keep_sem,
    give_sem,
):
    scaling = HEAD_DIM ** (-0.5)
    to_exp2 = scaling * LOG2E
    tall = (TK // 8, 8, TQ)
    core = lax.axis_index("dp") % 2
    group = (lax.axis_index("dp") // 2) * 2 + lax.axis_index("ctx") // 16
    per_piece = SEQ // TOK // PIECES

    def piece(n):
        at = pl.ds(n * per_piece, per_piece)
        return (
            pltpu.make_async_copy(z_ref.at[:, at, 0:64], qd_b.at[:, at], in_sem.at[n, 0]),
            pltpu.make_async_copy(z_ref.at[:, at, 64:96], kv_b.at[core, :, at], in_sem.at[n, 1]),
            pltpu.make_async_copy(other_ref.at[:, at], kv_b.at[1 - core, :, at], in_sem.at[n, 2]),
        )

    seg_copy = pltpu.make_async_copy(z_ref.at[group, :, 96:104], seg_b, seg_sem)
    seg_copy.start()
    pieces = [piece(n) for n in range(PIECES)]
    for copies in pieces:
        for copy in copies:
            copy.start()
    seg_copy.wait()

    ids = seg_b[...].astype(jnp.float32)
    cuts = [
        (jnp.sum((ids < float(doc)).astype(jnp.float32)) * 0.125).astype(jnp.int32)
        for doc in range(1, DOCS)
    ]

    lane = lax.broadcasted_iota(jnp.int32, (1, HEAD_DIM), 1)
    ends = jnp.zeros((1, HEAD_DIM), jnp.int32)
    for n, cut in enumerate(cuts):
        ends = jnp.where(lane == n, cut, ends)
    used = lane < DOCS - 1

    def lay_out(c, carry):
        at = pl.ds(pl.multiple_of(c * TOK, TOK), TOK)
        key_tile = kv_b[0, :, c].reshape(TOK, HEAD_DIM)
        value_tile = kv_b[1, :, c].reshape(TOK, HEAD_DIM)
        d_tile = qd_b[:, c, SHARE : 2 * SHARE, :].reshape(TOK, HEAD_DIM)
        q_s[at, :] = qd_b[:, c, 0:SHARE, :].reshape(TOK, HEAD_DIM)
        k_s[at, :] = key_tile
        v_s[at, :] = value_tile
        d_s[at, :] = d_tile
        kt_s[c] = key_tile.T
        vt_s[c] = value_tile.T
        dt_s[c] = d_tile.T
        spot = c * TOK + lax.broadcasted_iota(jnp.int32, (TOK, HEAD_DIM), 0)
        early = spot < ends
        qa_s[at, :] = jnp.where(used & ~early, NEG, 0.0).astype(jnp.bfloat16)
        ka_s[at, :] = jnp.where(used & early, 1.0, 0.0).astype(jnp.bfloat16)
        dk_s[at, :] = jnp.zeros((TOK, HEAD_DIM), jnp.float32)
        dv_s[at, :] = jnp.zeros((TOK, HEAD_DIM), jnp.float32)
        return carry

    for n in range(PIECES):
        for copy in pieces[n]:
            copy.wait()
        lax.fori_loop(n * per_piece, (n + 1) * per_piece, lay_out, 0, unroll=2)

    def doc_start(position):
        start = jnp.zeros_like(position)
        for cut in cuts:
            start = jnp.maximum(start, jnp.where(position >= cut, cut, 0))
        return start

    def chunks(i):
        first_row = i * TQ
        return doc_start(first_row) // TK, (first_row + TQ - 1) // TK + 1

    def key_at(j):
        return pl.ds(pl.multiple_of(j * TK, TK), TK)

    def query_at(i):
        return pl.ds(pl.multiple_of(i * TQ, TQ), TQ)

    def send_rows(i, n):
        at = pl.ds(i * (TQ // TOK), TQ // TOK)
        rows = slice(n * SHARE, n * SHARE + SHARE)
        return pltpu.make_async_copy(o_b.at[n, :, at], o_ref.at[:, at, rows], out_sem.at[n])

    def side_by_side(cols_s, first, count):
        return jnp.concatenate([cols_s[first + n] for n in range(count)], axis=1)

    def clear_forward():
        top_s[...] = jnp.full((8, TQ), NEG, jnp.float32)
        sum_s[...] = jnp.zeros((8, TQ), jnp.float32)
        ot_s[...] = jnp.zeros((HEAD_DIM, TQ), jnp.float32)

    def scores_of(i, j, p_s):
        k_at, q_at = key_at(j), query_at(i)
        keys = jnp.concatenate([k_s[k_at, :], ka_s[k_at, :]], axis=1)
        scores = dot_nt(keys, jnp.concatenate([q_s[q_at, :], qa_s[q_at, :]], axis=1))
        rows = i * TQ - j * TK + lax.broadcasted_iota(jnp.int32, (1, TQ), 1)
        keys = lax.broadcasted_iota(jnp.int32, (TK, TQ), 0)
        return jnp.where(keys <= rows, scores, NEG).reshape(tall)

    def soften(scores, j, p_s, tops_s):
        before = top_s[...]
        here = jnp.max(jnp.max(scores, axis=0), axis=0, keepdims=True)
        top = jnp.maximum(before, jnp.broadcast_to(here, (8, TQ)))
        part = jnp.exp2((scores - top) * to_exp2)
        fade = jnp.exp2((before - top) * to_exp2)
        sum_s[...] = sum_s[...] * fade + jnp.sum(part, axis=0)
        top_s[...] = top
        tops_s[j] = top
        part = part.reshape(TK, TQ)
        p_s[key_at(j), :] = part
        return part.astype(jnp.bfloat16), fade

    def add_out(j, part, fade):
        faded = (ot_s[...].reshape(HEAD_DIM // 8, 8, TQ) * fade).reshape(HEAD_DIM, TQ)
        ot_s[...] = faded + dot(side_by_side(vt_s, j * (TK // TOK), TK // TOK), part)

    def forward_step(i, j, p_s, tops_s):
        part, fade = soften(scores_of(i, j, p_s), j, p_s, tops_s)
        add_out(j, part, fade)

    def both_steps(i, j, p_s, tops_s, i_now, j_now, p_now, tops_now, rows_now):
        scores = scores_of(i, j, p_s)
        k_at, q_at = key_at(j_now), query_at(i_now)
        dprobs = dot_nt(v_s[k_at, :], d_s[q_at, :]).reshape(tall)
        share = jnp.exp2((tops_now[j_now] - rows_now[0]) * to_exp2) * rows_now[1]
        held = p_now[k_at, :].reshape(tall)
        weights = (held * share).reshape(TK, TQ).astype(jnp.bfloat16)
        dv_s[k_at, :] += dot(weights, d_s[q_at, :])
        part, fade = soften(scores, j, p_s, tops_s)
        dscore = (held * (share * scaling)) * (dprobs - rows_now[2])
        dscore = dscore.reshape(TK, TQ).astype(jnp.bfloat16)
        dk_s[k_at, :] += dot(dscore, q_s[q_at, :])
        qg_s[...] += dot(side_by_side(kt_s, j_now * (TK // TOK), TK // TOK), dscore)
        add_out(j, part, fade)

    def forward_end(i, rows_s):
        share = 1.0 / jnp.sum(sum_s[...], axis=0, keepdims=True)
        out_t = ot_s[...] * share
        dt = side_by_side(dt_s, i * (TQ // TOK), TQ // TOK)
        row_dot = jnp.sum(dt.astype(jnp.float32) * out_t, axis=0, keepdims=True)
        rows_s[0] = top_s[...]
        rows_s[1] = jnp.broadcast_to(share, (8, TQ))
        rows_s[2] = jnp.broadcast_to(row_dot, (8, TQ))
        out_rows = out_t.astype(jnp.bfloat16).T
        for n in range(TQ // TOK):
            tile = out_rows[n * TOK : n * TOK + TOK].reshape(4, SHARE, HEAD_DIM)
            o_b[0, :, i * (TQ // TOK) + n] = tile
        send_rows(i, 0).start()
        clear_forward()

    def gradient_step(i, j, p_s, tops_s, rows_s):
        k_at, q_at = key_at(j), query_at(i)
        share = jnp.exp2((tops_s[j] - rows_s[0]) * to_exp2) * rows_s[1]
        dprobs = dot_nt(v_s[k_at, :], d_s[q_at, :]).reshape(tall)
        part = p_s[k_at, :].reshape(tall)
        weights = (part * share).reshape(TK, TQ).astype(jnp.bfloat16)
        dv_s[k_at, :] += dot(weights, d_s[q_at, :])
        dscore = (part * (share * scaling)) * (dprobs - rows_s[2])
        dscore = dscore.reshape(TK, TQ).astype(jnp.bfloat16)
        dk_s[k_at, :] += dot(dscore, q_s[q_at, :])
        qg_s[...] += dot(side_by_side(kt_s, j * (TK // TOK), TK // TOK), dscore)

    def gradient_end(i):
        grad_rows = qg_s[...].astype(jnp.bfloat16).T
        for n in range(TQ // TOK):
            tile = grad_rows[n * TOK : n * TOK + TOK].reshape(4, SHARE, HEAD_DIM)
            o_b[1, :, i * (TQ // TOK) + n] = tile
        send_rows(i, 1).start()
        qg_s[...] = jnp.zeros((HEAD_DIM, TQ), jnp.float32)

    even = (p_even, tops_even, rows_even)
    odd = (p_odd, tops_odd, rows_odd)

    def stage(i_next, ahead, i_now, behind):
        now_lo, now_hi = chunks(i_now)
        next_lo, next_hi = chunks(jnp.minimum(i_next, SEQ // TQ - 1))
        next_n = jnp.where(i_next < SEQ // TQ, next_hi - next_lo, 0)
        now_n = now_hi - now_lo
        both = jnp.minimum(next_n, now_n)

        def together(t, carry):
            both_steps(i_next, next_lo + t, *ahead[:2], i_now, now_lo + t, *behind)
            return carry

        def ahead_only(t, carry):
            forward_step(i_next, next_lo + t, *ahead[:2])
            return carry

        def behind_only(t, carry):
            gradient_step(i_now, now_lo + t, *behind)
            return carry

        lax.fori_loop(0, both, together, 0)
        lax.fori_loop(both, next_n, ahead_only, 0)
        lax.fori_loop(both, now_n, behind_only, 0)

        @pl.when(i_next < SEQ // TQ)
        def _():
            forward_end(i_next, ahead[2])

        gradient_end(i_now)

    clear_forward()
    qg_s[...] = jnp.zeros((HEAD_DIM, TQ), jnp.float32)
    forward_step(0, 0, *even[:2])
    forward_end(0, rows_even)

    def two_stages(m, carry):
        stage(2 * m + 1, odd, 2 * m, even)
        stage(2 * m + 2, even, 2 * m + 1, odd)
        return carry

    lax.fori_loop(0, SEQ // TQ // 2, two_stages, 0)

    def give_back(c, carry):
        at = pl.ds(pl.multiple_of(c * TOK, TOK), TOK)
        kv_b[0, :, c] = dk_s[at, :].astype(jnp.bfloat16).reshape(4, SHARE, HEAD_DIM)
        kv_b[1, :, c] = dv_s[at, :].astype(jnp.bfloat16).reshape(4, SHARE, HEAD_DIM)
        return carry

    lax.fori_loop(0, SEQ // TOK, give_back, 0, unroll=2)
    keep_copy = pltpu.make_async_copy(kv_b.at[core], keep_ref, keep_sem)
    give_copy = pltpu.make_async_copy(kv_b.at[1 - core], give_ref, give_sem)
    keep_copy.start()
    give_copy.start()
    for n in range(2):
        rows = slice(n * SHARE, n * SHARE + SHARE)
        pltpu.make_async_copy(o_b.at[n], o_ref.at[:, :, rows], out_sem.at[n]).wait()
    keep_copy.wait()
    give_copy.wait()


def attention(z, other):
    tall = pltpu.VMEM((SEQ, HEAD_DIM), jnp.bfloat16)
    flat = pltpu.VMEM((SEQ // TOK, TOK, HEAD_DIM), jnp.bfloat16)
    anywhere = pl.BlockSpec(memory_space=pltpu.HBM)
    part = jax.ShapeDtypeStruct((4, 32, SHARE, HEAD_DIM), jnp.bfloat16)
    return pl.pallas_call(
        attention_kernel,
        in_specs=[anywhere, anywhere],
        out_specs=[anywhere, anywhere, anywhere],
        out_shape=[jax.ShapeDtypeStruct((4, 32, OUT_ROWS, HEAD_DIM), jnp.bfloat16), part, part],
        scratch_shapes=[
            pltpu.VMEM((4, 32, 2 * SHARE, HEAD_DIM), jnp.bfloat16),
            pltpu.VMEM((2, 4, 32, SHARE, HEAD_DIM), jnp.bfloat16),
            pltpu.VMEM((32, 8, HEAD_DIM), jnp.bfloat16),
            pltpu.VMEM((2, 4, 32, SHARE, HEAD_DIM), jnp.bfloat16),
        ]
        + [tall] * 6
        + [flat] * 3
        + [pltpu.VMEM((SEQ, TQ), jnp.float32)] * 2
        + [pltpu.VMEM((SEQ // TK, 8, TQ), jnp.float32)] * 2
        + [pltpu.VMEM((3, 8, TQ), jnp.float32)] * 2
        + [pltpu.VMEM((SEQ, HEAD_DIM), jnp.float32)] * 2
        + [pltpu.VMEM((HEAD_DIM, TQ), jnp.float32)] * 2
        + [pltpu.VMEM((8, TQ), jnp.float32)] * 2
        + [
            pltpu.SemaphoreType.DMA((PIECES, 3)),
            pltpu.SemaphoreType.DMA,
            pltpu.SemaphoreType.DMA((2,)),
            pltpu.SemaphoreType.DMA,
            pltpu.SemaphoreType.DMA,
        ],
        compiler_params=pltpu.CompilerParams(vmem_limit_bytes=56 << 20),
        name="attention",
    )(z, other)


def join_kernel(o_ref, keep_ref, got_ref, out_ref):
    both = keep_ref[...].astype(jnp.float32) + got_ref[...].astype(jnp.float32)
    out_ref[...] = both.astype(jnp.bfloat16)


def join(rows, keep, got):
    part = pl.BlockSpec((4, 8, SHARE, HEAD_DIM), lambda c: (0, c, 0, 0))
    return pl.pallas_call(
        join_kernel,
        grid=(4,),
        in_specs=[pl.BlockSpec(memory_space=pltpu.HBM), part, part],
        out_specs=pl.BlockSpec((4, 8, SHARE, HEAD_DIM), lambda c: (0, c, 2, 0)),
        out_shape=jax.ShapeDtypeStruct(rows.shape, rows.dtype),
        input_output_aliases={0: 0},
        name="join",
    )(rows, keep, got)


def to_other_core(x):
    return lax.ppermute(x, "dp", [(0, 1), (1, 0), (2, 3), (3, 2)])


def on_device(queries, key_proj, value_proj, out_grad, row_plan, segments):
    sent = pack(queries, key_proj, value_proj, out_grad, row_plan, segments)
    here = lax.all_to_all(
        sent.reshape(TOK, IN_ROWS, HEAD_DIM), ("dp", "ctx"), split_axis=0, concat_axis=0, tiled=True
    ).reshape(4, 32, IN_ROWS, HEAD_DIM)
    other = to_other_core(here[:, :, 64:96, :])
    rows, keep, give = attention(here, other)
    done = join(rows, keep, to_other_core(give))
    back = lax.all_to_all(
        done.reshape(TOK, OUT_ROWS, HEAD_DIM), ("dp", "ctx"), split_axis=0, concat_axis=0, tiled=True
    )
    return tuple(unpack(back.reshape(2, 2, 2, 16, OUT_ROWS, HEAD_DIM), row_plan))


def solution(mesh):
    rows = P(("dp", "ctx"), None)
    return jax.shard_map(
        on_device,
        mesh=mesh,
        in_specs=(rows, rows, rows, rows, P(("dp", "ctx")), P("dp", "ctx")),
        out_specs=(rows, rows, rows, rows),
        check_vma=False,
    )
```

time: 186 us -> 163 us (0.88)
  waiting for transfers between devices: 56.8 us -> 4.79 us
  blocking collectives: 58.7 us -> 103 us
  starting transfers between devices: 11.9 us -> 0.93 us
  Pallas kernels: 56.6 us -> 49.1 us
  local copies, waits for them, and re-layouts: 0 us -> 2.03 us
    all_to_all x1 -> x0, waiting for transfers between devices: 56.8 us -> none  [on_device(): lax.all_to_all(sent.reshape(TOK, IN_ROWS, HEAD_DIM), ('dp', 'ctx'), split...]
    all_to_all x0 -> x1, blocking collectives: none -> 56.4 us  [on_device(): lax.all_to_all(sent.reshape(TOK, IN_ROWS, HEAD_DIM), ('dp', 'ctx'), split...]
    all_to_all x1 -> x0, starting transfers between devices: 11.9 us -> none  [on_device(): lax.all_to_all(sent.reshape(TOK, IN_ROWS, HEAD_DIM), ('dp', 'ctx'), split...]
    all_to_all x1, blocking collectives: 58.7 us -> 47 us  [on_device(): lax.all_to_all(done.reshape(TOK, OUT_ROWS, HEAD_DIM), ('dp', 'ctx'), spli...]
    pallas_call x1 -> x2, Pallas kernels: 46.9 us -> 39.8 us  [the longest x1 36.1 us: attention(): pl.pallas_call(attention_kernel, in_specs=[anywhere, anywhere], out_specs...]
    ppermute x0 -> x2, waiting for transfers between devices: none -> 4.79 us  [to_other_core(): return lax.ppermute(x, 'dp', [(0, 1), (1, 0), (2, 3), (3, 2)])]
    unnamed x0 -> x6, local copies, waits for them, and re-layouts: none -> 1.94 us
  transfers between devices with their start and end apart: 1 -> 2, of which waited for: 1 -> 2; matrix products, arithmetic and copies ran while one was open for 0% -> 0% of each run, Pallas kernels for 0% -> 0%
where the time goes in v2:
time: 163 us; the launch traced here: 161 us
  blocking collectives  103 us (63%)
  Pallas kernels  49.1 us (30%)
  waiting for transfers between devices  4.79 us (3%)
  local copies, waits for them, and re-layouts  2.03 us (1%)
    all_to_all x1, blocking collectives, on_device(): lax.all_to_all(sent.reshape(TOK, IN_ROWS, HEAD_DIM), ('dp', 'ctx'), split...  56.4 us
    all_to_all x1, blocking collectives, on_device(): lax.all_to_all(done.reshape(TOK, OUT_ROWS, HEAD_DIM), ('dp', 'ctx'), spli...  47 us
    pallas_call x1, Pallas kernels, attention(): pl.pallas_call(attention_kernel, in_specs=[anywhere, anywhere], out_specs...  36.1 us
    pallas_call x1, Pallas kernels, pack(): pl.pallas_call(pack_kernel, grid=(KV_HEADS,), in_specs=[pl.BlockSpec((1,...  4.8 us
    ppermute x2, waiting for transfers between devices, to_other_core(): return lax.ppermute(x, 'dp', [(0, 1), (1, 0), (2, 3), (3, 2)])  4.79 us
    pallas_call x1, Pallas kernels, unpack(): pl.pallas_call(unpack_kernel, grid=(KV_HEADS,), in_specs=[pl.BlockSpec((1...  4.55 us
    pallas_call x1, Pallas kernels, join(): pl.pallas_call(join_kernel, grid=(4,), in_specs=[pl.BlockSpec(memory_spac...  3.67 us
  transfers between devices with their start and end apart: 2, of which 2 were waited for; matrix products, arithmetic and copies ran while one was open for 0% of the time, Pallas kernels for 0%

profile of v2, /device:TPU:1, one launch (start us, length us, event | category | flops | bytes accessed | tf_op | source)
XLA Modules:
  0.0 160.9 jit_solution(16905374791222483083)
XLA Ops:
  0.6 4.8 %pack.1 = bf16[2,2,2,16,104,128]{5,4,3,2,1,0:T(8,128)(2,1)} custom-call(s32[1,128]{1,0:T(1,128)} %bitcast.10, s32[1,128]{1,0:T(1,128)} %seg_ref.1, bf16[128,4096]{1,0:T(8,128)(2,1)} %q_ref.1, bf16[128,4096]{1,0:T(8,128)(2,1)} %d_ref.1, bf16[128,512]{1,0:T(8,128)(2,1)} %k_ref.1, bf16[128,512]{1,0:T(8,128)(2,1)} %v_ref.1), custom_call_target="tpu_custom_call" | custom-call | tf_op jit(solution)/shard_map/pack/pallas_call | solution.py:63
  5.4 56.4 %all_to_all.10 = bf16[128,104,128]{2,1,0:T(8,128)(2,1)S(1)} all-to-all(bf16[128,104,128]{2,1,0:T(8,128)(2,1)} %bitcast.7), channel_id=1, replica_groups=mesh['dp'=4,'ctx'=32] {'dp','ctx'}, dimensions={0} | all-to-all | bytes 6815744 | tf_op jit(solution)/shard_map/all_to_all | solution.py:458
  61.9 0.0 copy-start
  61.9 0.1 slice.4
  61.9 0.5 collective-permute-start
  62.4 2.3 %collective-permute-done.other_ref = bf16[4,32,32,128]{3,2,1,0:T(8,128)(2,1)S(1)} collective-permute-done((bf16[4,32,32,128]{3,2,1,0:T(8,128)(2,1)S(1)}, bf16[4,32,32,128]{3,2,1,0:T(8,128)(2,1)S(1)}, u32[]{:S(2)}, u32[]{:S(2)}) %collective-permute-start) | collective-permute-done | bytes 1048608 | tf_op jit(solution)/shard_map/ppermute | solution.py:453
  64.7 0.0 copy-done
  64.7 0.0 copy-start.1
  64.7 1.0 copy-done.1
  65.7 36.1 %attention.1 = (bf16[4,32,96,128]{3,2,1,0:T(8,128)(2,1)}, bf16[4,32,32,128]{3,2,1,0:T(8,128)(2,1)}, bf16[4,32,32,128]{3,2,1,0:T(8,128)(2,1)}) custom-call(bf16[4,32,104,128]{3,2,1,0:T(8,128)(2,1)} %bitcast.6, bf16[4,32,32,128]{3,2,1,0:T(8,128)(2,1)} %copy-done.1), custom_call_target="tpu_custom_call" | custom-call | tf_op jit(solution)/shard_map/attention/pallas_call | solution.py:403
  101.8 0.5 collective-permute-start.1
  102.2 2.5 %collective-permute-done.1.got_ref = bf16[4,32,32,128]{3,2,1,0:T(8,128)(2,1)S(1)} collective-permute-done((bf16[4,32,32,128]{3,2,1,0:T(8,128)(2,1)}, bf16[4,32,32,128]{3,2,1,0:T(8,128)(2,1)S(1)}, u32[]{:S(2)}, u32[]{:S(2)}) %collective-permute-start.1) | collective-permute-done | bytes 1048608 | tf_op jit(solution)/shard_map/ppermute | solution.py:453
  104.7 0.0 copy-start.2
  104.7 1.0 copy-done.2
  105.7 3.7 %join.1 = bf16[4,32,96,128]{3,2,1,0:T(8,128)(2,1)} custom-call(bf16[4,32,96,128]{3,2,1,0:T(8,128)(2,1)} %get-tuple-element.7.o_ref, bf16[4,32,32,128]{3,2,1,0:T(8,128)(2,1)} %get-tuple-element.8.keep_ref, bf16[4,32,32,128]{3,2,1,0:T(8,128)(2,1)} %copy-done.2), custom_call_target="tpu_custom_call", output_to_operand_aliasing={{}: (0, {})} | custom-call | tf_op jit(solution)/shard_map/join/pallas_call | solution.py:441
  109.4 47.0 %all_to_all.11 = bf16[128,96,128]{2,1,0:T(8,128)(2,1)} all-to-all(bf16[128,96,128]{2,1,0:T(8,128)(2,1)} %bitcast.9), channel_id=1, replica_groups=mesh['dp'=4,'ctx'=32] {'dp','ctx'}, dimensions={0} | all-to-all | bytes 6291456 | tf_op jit(solution)/shard_map/all_to_all | solution.py:464
  156.4 4.5 %unpack.1 = (bf16[128,4096]{1,0:T(8,128)(2,1)}, bf16[128,4096]{1,0:T(8,128)(2,1)}, bf16[128,512]{1,0:T(8,128)(2,1)}, bf16[128,512]{1,0:T(8,128)(2,1)}) custom-call(s32[1,128]{1,0:T(1,128)} %bitcast.11, bf16[2,2,2,16,96,128]{5,4,3,2,1,0:T(8,128)(2,1)} %bitcast.8), custom_call_target="tpu_custom_call" | custom-call | tf_op jit(solution)/shard_map/unpack/pallas_call | solution.py:106
Async XLA Ops:
  61.9 2.9 %copy-start = (bf16[128,104,128]{2,1,0:T(8,128)(2,1)}, bf16[128,104,128]{2,1,0:T(8,128)(2,1)S(1)}, u32[]{:S(2)}) copy-start(bf16[128,104,128]{2,1,0:T(8,128)(2,1)S(1)} %all_to_all.10) | copy-start | bytes 10223620
  61.9 2.8 %collective-permute-start = (bf16[4,32,32,128]{3,2,1,0:T(8,128)(2,1)S(1)}, bf16[4,32,32,128]{3,2,1,0:T(8,128)(2,1)S(1)}, u32[]{:S(2)}, u32[]{:S(2)}) collective-permute-start(bf16[4,32,32,128]{3,2,1,0:T(8,128)(2,1)S(1)} %slice.4), channel_id=1, source_target_pairs={{0,32},{32,0},{64,96},{96,64},{1,33},{33,1},{65,97},{97,65},{2,34}... | collective-permute-start | bytes 3145736 | tf_op jit(solution)/shard_map/ppermute | solution.py:453
  64.7 1.0 copy-start.1
  101.8 3.0 %collective-permute-start.1 = (bf16[4,32,32,128]{3,2,1,0:T(8,128)(2,1)}, bf16[4,32,32,128]{3,2,1,0:T(8,128)(2,1)S(1)}, u32[]{:S(2)}, u32[]{:S(2)}) collective-permute-start(bf16[4,32,32,128]{3,2,1,0:T(8,128)(2,1)} %get-tuple-element.9), channel_id=1, source_target_pairs={{0,32},{32,0},{64,96},{96,64},{1,33},{33,1},{65,97},{97,65},{2,34}... | collective-permute-start | bytes 3145736 | tf_op jit(solution)/shard_map/ppermute | solution.py:453
  104.7 1.0 copy-start.2

commit v3 on v2

--- a/solution.py
+++ b/solution.py
@@ -22,7 +22,6 @@
 
 IN_ROWS = 3 * SHARE + 8
 OUT_ROWS = 3 * SHARE
-PIECES = 4
 
 
 def dot(a, b):
@@ -38,53 +37,107 @@
     return jnp.where(rows == plan_ref[...], 1.0, 0.0).astype(jnp.float32)
 
 
-def pack_kernel(plan_ref, seg_ref, q_ref, d_ref, k_ref, v_ref, o_ref):
+def pack_kernel(
+    plan_hbm,
+    seg_hbm,
+    q_hbm,
+    d_hbm,
+    k_hbm,
+    v_hbm,
+    o_ref,
+    plan_ref,
+    seg_ref,
+    q_ref,
+    d_ref,
+    k_ref,
+    v_ref,
+    sems,
+):
+    small = [
+        pltpu.make_async_copy(plan_hbm, plan_ref, sems.at[0]),
+        pltpu.make_async_copy(k_hbm, k_ref, sems.at[1]),
+        pltpu.make_async_copy(v_hbm, v_ref, sems.at[2]),
+        pltpu.make_async_copy(seg_hbm, seg_ref, sems.at[3]),
+    ]
+    for copy in small:
+        copy.start()
+    large = []
+    for g in range(KV_HEADS):
+        at = pl.ds(g * GROUPS * HEAD_DIM, GROUPS * HEAD_DIM)
+        large.append(
+            (
+                pltpu.make_async_copy(q_hbm.at[:, at], q_ref.at[:, at], sems.at[4 + 2 * g]),
+                pltpu.make_async_copy(d_hbm.at[:, at], d_ref.at[:, at], sems.at[5 + 2 * g]),
+            )
+        )
+        for copy in large[g]:
+            copy.start()
+    for copy in small:
+        copy.wait()
     pick = plan_matrix(plan_ref).T.astype(jnp.bfloat16)
     seg_rows = jnp.broadcast_to(seg_ref[...].astype(jnp.float32), (8, TOK)).astype(jnp.bfloat16)
-    k_rows = dot(pick, k_ref[...]).astype(jnp.bfloat16)
-    v_rows = dot(pick, v_ref[...]).astype(jnp.bfloat16)
-    for pair in range(GROUPS // 2):
-        at = slice(pair * 256, pair * 256 + 256)
-        q_rows = dot(pick, q_ref[:, at]).astype(jnp.bfloat16)
-        d_rows = dot(pick, d_ref[:, at]).astype(jnp.bfloat16)
-        for core in range(2):
-            cols = slice(core * HEAD_DIM, core * HEAD_DIM + HEAD_DIM)
-            for b in range(4):
-                rows = slice(b * SHARE, b * SHARE + SHARE)
-                to = (b // 2, core, b % 2, pair)
-                o_ref[to + (slice(0, 32),)] = q_rows[rows, cols]
-                o_ref[to + (slice(32, 64),)] = d_rows[rows, cols]
-                o_ref[to + (slice(64, 96),)] = (k_rows, v_rows)[core][rows, :]
-                o_ref[to + (slice(96, 104),)] = seg_rows
+    for g in range(KV_HEADS):
+        cols = slice(g * HEAD_DIM, g * HEAD_DIM + HEAD_DIM)
+        k_rows = dot(pick, k_ref[:, cols]).astype(jnp.bfloat16)
+        v_rows = dot(pick, v_ref[:, cols]).astype(jnp.bfloat16)
+        for pair in range(GROUPS // 2):
+            for core in range(2):
+                for b in range(4):
+                    rows = slice(b * SHARE, b * SHARE + SHARE)
+                    o_ref[b // 2, core, b % 2, g * (GROUPS // 2) + pair, 64:96] = (k_rows, v_rows)[
+                        core
+                    ][rows]
+                    o_ref[b // 2, core, b % 2, g * (GROUPS // 2) + pair, 96:104] = seg_rows
+        for n, (copy, ref) in enumerate(zip(large[g], (q_ref, d_ref))):
+            copy.wait()
+            for pair in range(GROUPS // 2):
+                first = (g * (GROUPS // 2) + pair) * 2 * HEAD_DIM
+                both = dot(pick, ref[:, first : first + 2 * HEAD_DIM]).astype(jnp.bfloat16)
+                for core in range(2):
+                    cols = slice(core * HEAD_DIM, core * HEAD_DIM + HEAD_DIM)
+                    for b in range(4):
+                        rows = slice(b * SHARE, b * SHARE + SHARE)
+                        to = slice(n * SHARE, n * SHARE + SHARE)
+                        o_ref[b // 2, core, b % 2, g * (GROUPS // 2) + pair, to] = both[rows, cols]
 
 
 def pack(queries, key_proj, value_proj, out_grad, row_plan, segments):
-    wide = GROUPS * HEAD_DIM
+    outside = pl.BlockSpec(memory_space=pltpu.HBM)
+    outside_args = (
+        row_plan.reshape(1, TOK),
+        segments,
+        queries,
+        out_grad,
+        key_proj,
+        value_proj,
+    )
     return pl.pallas_call(
         pack_kernel,
-        grid=(KV_HEADS,),
-        in_specs=[
-            pl.BlockSpec((1, TOK), lambda g: (0, 0)),
-            pl.BlockSpec((1, TOK), lambda g: (0, 0)),
-            pl.BlockSpec((TOK, wide), lambda g: (0, g)),
-            pl.BlockSpec((TOK, wide), lambda g: (0, g)),
-            pl.BlockSpec((TOK, HEAD_DIM), lambda g: (0, g)),
-            pl.BlockSpec((TOK, HEAD_DIM), lambda g: (0, g)),
+        in_specs=[outside] * 6,
+        out_specs=pl.BlockSpec(memory_space=pltpu.VMEM),
+        out_shape=jax.ShapeDtypeStruct((2, 2, 2, 16, IN_ROWS, HEAD_DIM), jnp.bfloat16),
+        scratch_shapes=[
+            pltpu.VMEM((1, TOK), jnp.int32),
+            pltpu.VMEM((1, TOK), jnp.int32),
+            pltpu.VMEM(queries.shape, queries.dtype),
+            pltpu.VMEM(out_grad.shape, out_grad.dtype),
+            pltpu.VMEM(key_proj.shape, key_proj.dtype),
+            pltpu.VMEM(value_proj.shape, value_proj.dtype),
+            pltpu.SemaphoreType.DMA((4 + 2 * KV_HEADS,)),
         ],
-        out_specs=pl.BlockSpec(
-            (2, 2, 2, GROUPS // 2, IN_ROWS, HEAD_DIM), lambda g: (0, 0, 0, g, 0, 0)
-        ),
-        out_shape=jax.ShapeDtypeStruct((2, 2, 2, 16, IN_ROWS, HEAD_DIM), jnp.bfloat16),
+        compiler_params=pltpu.CompilerParams(vmem_limit_bytes=16 << 20),
         name="pack",
-    )(row_plan.reshape(1, TOK), segments, queries, out_grad, key_proj, value_proj)
+    )(*(pltpu.with_memory_space_constraint(x, pltpu.HBM) for x in outside_args))
 
 
 def unpack_kernel(plan_ref, y_ref, att_ref, qg_ref, kg_ref, vg_ref):
     put = plan_matrix(plan_ref).astype(jnp.bfloat16)
 
+    base = pl.program_id(0) * (GROUPS // 2)
+
     def slots(core, pair, first):
         parts = [
-            y_ref[b // 2, core, b % 2, pair, slice(first, first + SHARE)] for b in range(4)
+            y_ref[b // 2, core, b % 2, base + pair, slice(first, first + SHARE)] for b in range(4)
         ]
         return jnp.concatenate(parts, axis=0)
 
@@ -108,9 +161,7 @@
         grid=(KV_HEADS,),
         in_specs=[
             pl.BlockSpec((1, TOK), lambda g: (0, 0)),
-            pl.BlockSpec(
-                (2, 2, 2, GROUPS // 2, OUT_ROWS, HEAD_DIM), lambda g: (0, 0, 0, g, 0, 0)
-            ),
+            pl.BlockSpec(memory_space=pltpu.VMEM),
         ],
         out_specs=[
             pl.BlockSpec((TOK, wide), lambda g: (0, g)),
@@ -124,6 +175,7 @@
             jax.ShapeDtypeStruct((TOK, KV_HEADS * HEAD_DIM), jnp.bfloat16),
             jax.ShapeDtypeStruct((TOK, KV_HEADS * HEAD_DIM), jnp.bfloat16),
         ],
+        compiler_params=pltpu.CompilerParams(vmem_limit_bytes=16 << 20),
         name="unpack",
     )(row_plan.reshape(1, TOK), back)
 
@@ -134,10 +186,6 @@
     o_ref,
     keep_ref,
     give_ref,
-    qd_b,
-    kv_b,
-    seg_b,
-    o_b,
     q_s,
     qa_s,
     d_s,
@@ -159,36 +207,14 @@
     qg_s,
     top_s,
     sum_s,
-    in_sem,
-    seg_sem,
-    out_sem,
-    keep_sem,
-    give_sem,
 ):
     scaling = HEAD_DIM ** (-0.5)
     to_exp2 = scaling * LOG2E
     tall = (TK // 8, 8, TQ)
     core = lax.axis_index("dp") % 2
     group = (lax.axis_index("dp") // 2) * 2 + lax.axis_index("ctx") // 16
-    per_piece = SEQ // TOK // PIECES
-
-    def piece(n):
-        at = pl.ds(n * per_piece, per_piece)
-        return (
-            pltpu.make_async_copy(z_ref.at[:, at, 0:64], qd_b.at[:, at], in_sem.at[n, 0]),
-            pltpu.make_async_copy(z_ref.at[:, at, 64:96], kv_b.at[core, :, at], in_sem.at[n, 1]),
-            pltpu.make_async_copy(other_ref.at[:, at], kv_b.at[1 - core, :, at], in_sem.at[n, 2]),
-        )
-
-    seg_copy = pltpu.make_async_copy(z_ref.at[group, :, 96:104], seg_b, seg_sem)
-    seg_copy.start()
-    pieces = [piece(n) for n in range(PIECES)]
-    for copies in pieces:
-        for copy in copies:
-            copy.start()
-    seg_copy.wait()
-
-    ids = seg_b[...].astype(jnp.float32)
+
+    ids = z_ref[group, :, 96:104].astype(jnp.float32)
     cuts = [
         (jnp.sum((ids < float(doc)).astype(jnp.float32)) * 0.125).astype(jnp.int32)
         for doc in range(1, DOCS)
@@ -202,10 +228,12 @@
 
     def lay_out(c, carry):
         at = pl.ds(pl.multiple_of(c * TOK, TOK), TOK)
-        key_tile = kv_b[0, :, c].reshape(TOK, HEAD_DIM)
-        value_tile = kv_b[1, :, c].reshape(TOK, HEAD_DIM)
-        d_tile = qd_b[:, c, SHARE : 2 * SHARE, :].reshape(TOK, HEAD_DIM)
-        q_s[at, :] = qd_b[:, c, 0:SHARE, :].reshape(TOK, HEAD_DIM)
+        mine = z_ref[:, c, 64:96, :].reshape(TOK, HEAD_DIM)
+        theirs = other_ref[:, c].reshape(TOK, HEAD_DIM)
+        key_tile = jnp.where(core == 0, mine, theirs)
+        value_tile = jnp.where(core == 0, theirs, mine)
+        d_tile = z_ref[:, c, SHARE : 2 * SHARE, :].reshape(TOK, HEAD_DIM)
+        q_s[at, :] = z_ref[:, c, 0:SHARE, :].reshape(TOK, HEAD_DIM)
         k_s[at, :] = key_tile
         v_s[at, :] = value_tile
         d_s[at, :] = d_tile
@@ -220,10 +248,7 @@
         dv_s[at, :] = jnp.zeros((TOK, HEAD_DIM), jnp.float32)
         return carry
 
-    for n in range(PIECES):
-        for copy in pieces[n]:
-            copy.wait()
-        lax.fori_loop(n * per_piece, (n + 1) * per_piece, lay_out, 0, unroll=2)
+    lax.fori_loop(0, SEQ // TOK, lay_out, 0, unroll=4)
 
     def doc_start(position):
         start = jnp.zeros_like(position)
@@ -240,11 +265,6 @@
 
     def query_at(i):
         return pl.ds(pl.multiple_of(i * TQ, TQ), TQ)
-
-    def send_rows(i, n):
-        at = pl.ds(i * (TQ // TOK), TQ // TOK)
-        rows = slice(n * SHARE, n * SHARE + SHARE)
-        return pltpu.make_async_copy(o_b.at[n, :, at], o_ref.at[:, at, rows], out_sem.at[n])
 
     def side_by_side(cols_s, first, count):
         return jnp.concatenate([cols_s[first + n] for n in range(count)], axis=1)
@@ -309,8 +329,7 @@
         out_rows = out_t.astype(jnp.bfloat16).T
         for n in range(TQ // TOK):
             tile = out_rows[n * TOK : n * TOK + TOK].reshape(4, SHARE, HEAD_DIM)
-            o_b[0, :, i * (TQ // TOK) + n] = tile
-        send_rows(i, 0).start()
+            o_ref[:, i * (TQ // TOK) + n, 0:32] = tile
         clear_forward()
 
     def gradient_step(i, j, p_s, tops_s, rows_s):
@@ -329,8 +348,7 @@
         grad_rows = qg_s[...].astype(jnp.bfloat16).T
         for n in range(TQ // TOK):
             tile = grad_rows[n * TOK : n * TOK + TOK].reshape(4, SHARE, HEAD_DIM)
-            o_b[1, :, i * (TQ // TOK) + n] = tile
-        send_rows(i, 1).start()
+            o_ref[:, i * (TQ // TOK) + n, 32:64] = tile
         qg_s[...] = jnp.zeros((HEAD_DIM, TQ), jnp.float32)
 
     even = (p_even, tops_even, rows_even)
@@ -379,72 +397,56 @@
 
     def give_back(c, carry):
         at = pl.ds(pl.multiple_of(c * TOK, TOK), TOK)
-        kv_b[0, :, c] = dk_s[at, :].astype(jnp.bfloat16).reshape(4, SHARE, HEAD_DIM)
-        kv_b[1, :, c] = dv_s[at, :].astype(jnp.bfloat16).reshape(4, SHARE, HEAD_DIM)
+        k_part = dk_s[at, :].astype(jnp.bfloat16)
+        v_part = dv_s[at, :].astype(jnp.bfloat16)
+        keep_ref[:, c] = jnp.where(core == 0, k_part, v_part).reshape(4, SHARE, HEAD_DIM)
+        give_ref[:, c] = jnp.where(core == 0, v_part, k_part).reshape(4, SHARE, HEAD_DIM)
         return carry
 
-    lax.fori_loop(0, SEQ // TOK, give_back, 0, unroll=2)
-    keep_copy = pltpu.make_async_copy(kv_b.at[core], keep_ref, keep_sem)
-    give_copy = pltpu.make_async_copy(kv_b.at[1 - core], give_ref, give_sem)
-    keep_copy.start()
-    give_copy.start()
-    for n in range(2):
-        rows = slice(n * SHARE, n * SHARE + SHARE)
-        pltpu.make_async_copy(o_b.at[n], o_ref.at[:, :, rows], out_sem.at[n]).wait()
-    keep_copy.wait()
-    give_copy.wait()
+    lax.fori_loop(0, SEQ // TOK, give_back, 0, unroll=4)
 
 
 def attention(z, other):
     tall = pltpu.VMEM((SEQ, HEAD_DIM), jnp.bfloat16)
     flat = pltpu.VMEM((SEQ // TOK, TOK, HEAD_DIM), jnp.bfloat16)
-    anywhere = pl.BlockSpec(memory_space=pltpu.HBM)
+    whole = pl.BlockSpec(memory_space=pltpu.VMEM)
     part = jax.ShapeDtypeStruct((4, 32, SHARE, HEAD_DIM), jnp.bfloat16)
     return pl.pallas_call(
         attention_kernel,
-        in_specs=[anywhere, anywhere],
-        out_specs=[anywhere, anywhere, anywhere],
-        out_shape=[jax.ShapeDtypeStruct((4, 32, OUT_ROWS, HEAD_DIM), jnp.bfloat16), part, part],
-        scratch_shapes=[
-            pltpu.VMEM((4, 32, 2 * SHARE, HEAD_DIM), jnp.bfloat16),
-            pltpu.VMEM((2, 4, 32, SHARE, HEAD_DIM), jnp.bfloat16),
-            pltpu.VMEM((32, 8, HEAD_DIM), jnp.bfloat16),
-            pltpu.VMEM((2, 4, 32, SHARE, HEAD_DIM), jnp.bfloat16),
-        ]
-        + [tall] * 6
+        in_specs=[whole, whole],
+        out_specs=[whole, whole, whole],
+        out_shape=[jax.ShapeDtypeStruct((4, 32, 2 * SHARE, HEAD_DIM), jnp.bfloat16), part, part],
+        scratch_shapes=[tall] * 6
         + [flat] * 3
         + [pltpu.VMEM((SEQ, TQ), jnp.float32)] * 2
         + [pltpu.VMEM((SEQ // TK, 8, TQ), jnp.float32)] * 2
         + [pltpu.VMEM((3, 8, TQ), jnp.float32)] * 2
         + [pltpu.VMEM((SEQ, HEAD_DIM), jnp.float32)] * 2
         + [pltpu.VMEM((HEAD_DIM, TQ), jnp.float32)] * 2
-        + [pltpu.VMEM((8, TQ), jnp.float32)] * 2
-        + [
-            pltpu.SemaphoreType.DMA((PIECES, 3)),
-            pltpu.SemaphoreType.DMA,
-            pltpu.SemaphoreType.DMA((2,)),
-            pltpu.SemaphoreType.DMA,
-            pltpu.SemaphoreType.DMA,
-        ],
-        compiler_params=pltpu.CompilerParams(vmem_limit_bytes=56 << 20),
+        + [pltpu.VMEM((8, TQ), jnp.float32)] * 2,
+        compiler_params=pltpu.CompilerParams(vmem_limit_bytes=36 << 20),
         name="attention",
     )(z, other)
 
 
-def join_kernel(o_ref, keep_ref, got_ref, out_ref):
-    both = keep_ref[...].astype(jnp.float32) + got_ref[...].astype(jnp.float32)
-    out_ref[...] = both.astype(jnp.bfloat16)
+def join_kernel(rows_ref, keep_ref, got_ref, out_ref):
+    def step(c, carry):
+        out_ref[:, c, 0:64] = rows_ref[:, c]
+        both = keep_ref[:, c].astype(jnp.float32) + got_ref[:, c].astype(jnp.float32)
+        out_ref[:, c, 64:96] = both.astype(jnp.bfloat16)
+        return carry
+
+    lax.fori_loop(0, 32, step, 0, unroll=4)
 
 
 def join(rows, keep, got):
-    part = pl.BlockSpec((4, 8, SHARE, HEAD_DIM), lambda c: (0, c, 0, 0))
+    whole = pl.BlockSpec(memory_space=pltpu.VMEM)
     return pl.pallas_call(
         join_kernel,
-        grid=(4,),
-        in_specs=[pl.BlockSpec(memory_space=pltpu.HBM), part, part],
-        out_specs=pl.BlockSpec((4, 8, SHARE, HEAD_DIM), lambda c: (0, c, 2, 0)),
-        out_shape=jax.ShapeDtypeStruct(rows.shape, rows.dtype),
-        input_output_aliases={0: 0},
+        in_specs=[whole] * 3,
+        out_specs=whole,
+        out_shape=jax.ShapeDtypeStruct((4, 32, OUT_ROWS, HEAD_DIM), jnp.bfloat16),
+        compiler_params=pltpu.CompilerParams(vmem_limit_bytes=16 << 20),
         name="join",
     )(rows, keep, got)
 

time: 163 us -> 151 us (0.926); the launches traced: 161 us -> 152 us
  Pallas kernels: 49.1 us -> 44.5 us
  local copies, waits for them, and re-layouts: 2.03 us -> 0.09 us
    pallas_call x3, Pallas kernels: 44.6 us -> 41.9 us  [the longest x1 38.5 us: attention(): pl.pallas_call(attention_kernel, in_specs=[whole, whole], out_specs=[whol...]
    pallas_call x1, Pallas kernels: 4.55 us -> 2.57 us  [unpack(): pl.pallas_call(unpack_kernel, grid=(KV_HEADS,), in_specs=[pl.BlockSpec((1...]
    unnamed x6 -> x2, local copies, waits for them, and re-layouts: 1.94 us -> 0.01 us
    all_to_all x1, blocking collectives: 47 us -> 45.3 us  [on_device(): lax.all_to_all(done.reshape(TOK, OUT_ROWS, HEAD_DIM), ('dp', 'ctx'), spli...]
where the time goes in v3:
time: 151 us; the launch traced here: 152 us
  blocking collectives  102 us (68%)
  Pallas kernels  44.5 us (29%)
  waiting for transfers between devices  4.58 us (3%)
    all_to_all x1, blocking collectives, on_device(): lax.all_to_all(sent.reshape(TOK, IN_ROWS, HEAD_DIM), ('dp', 'ctx'), split...  56.2 us
    all_to_all x1, blocking collectives, on_device(): lax.all_to_all(done.reshape(TOK, OUT_ROWS, HEAD_DIM), ('dp', 'ctx'), spli...  45.3 us
    pallas_call x1, Pallas kernels, attention(): pl.pallas_call(attention_kernel, in_specs=[whole, whole], out_specs=[whol...  38.5 us
    ppermute x2, waiting for transfers between devices, to_other_core(): return lax.ppermute(x, 'dp', [(0, 1), (1, 0), (2, 3), (3, 2)])  4.58 us
    pallas_call x1, Pallas kernels, pack(): pl.pallas_call(pack_kernel, in_specs=[outside] * 6, out_specs=pl.BlockSpe...  3.14 us
  transfers between devices with their start and end apart: 2, of which 2 were waited for; matrix products, arithmetic and copies ran while one was open for 0% of the time, Pallas kernels for 0%

profile of v3, /device:TPU:1, one launch (start us, length us, event | category | flops | bytes accessed | tf_op | source)
XLA Modules:
  0.0 152.3 jit_solution(8722451469919407074)
XLA Ops:
  0.6 3.1 %pack.1 = bf16[2,2,2,16,104,128]{5,4,3,2,1,0:T(8,128)(2,1)S(1)} custom-call(s32[1,128]{1,0:T(1,128)} %bitcast.10, s32[1,128]{1,0:T(1,128)} %seg_hbm.1, bf16[128,4096]{1,0:T(8,128)(2,1)} %q_hbm.1, bf16[128,4096]{1,0:T(8,128)(2,1)} %d_hbm.1, bf16[128,512]{1,0:T(8,128)(2,1)} %k_hbm.1, bf16[128,512]{1,0:T(8,128)(2,1)} %v_hbm.1), custom_call_target="tpu_custom_call" | custom-call | tf_op jit(solution)/shard_map/pack/pallas_call | solution.py:114
  3.8 56.2 %all_to_all.10 = bf16[128,104,128]{2,1,0:T(8,128)(2,1)S(1)} all-to-all(bf16[128,104,128]{2,1,0:T(8,128)(2,1)S(1)} %bitcast.7), channel_id=1, replica_groups=mesh['dp'=4,'ctx'=32] {'dp','ctx'}, dimensions={0} | all-to-all | bytes 6815744 | tf_op jit(solution)/shard_map/all_to_all | solution.py:460
  60.0 0.1 slice.4
  60.1 0.5 collective-permute-start
  60.6 2.3 %collective-permute-done.other_ref = bf16[4,32,32,128]{3,2,1,0:T(8,128)(2,1)S(1)} collective-permute-done((bf16[4,32,32,128]{3,2,1,0:T(8,128)(2,1)S(1)}, bf16[4,32,32,128]{3,2,1,0:T(8,128)(2,1)S(1)}, u32[]{:S(2)}, u32[]{:S(2)}) %collective-permute-start) | collective-permute-done | bytes 1048608 | tf_op jit(solution)/shard_map/ppermute | solution.py:455
  62.9 38.5 %attention.1 = (bf16[4,32,64,128]{3,2,1,0:T(8,128)(2,1)S(1)}, bf16[4,32,32,128]{3,2,1,0:T(8,128)(2,1)S(1)}, bf16[4,32,32,128]{3,2,1,0:T(8,128)(2,1)S(1)}) custom-call(bf16[4,32,104,128]{3,2,1,0:T(8,128)(2,1)S(1)} %bitcast.6, bf16[4,32,32,128]{3,2,1,0:T(8,128)(2,1)S(1)} %collective-permute-done.other_ref), custom_call_target="tpu_custom_call" | custom-call | tf_op jit(solution)/shard_map/attention/pallas_call | solution.py:414
  101.4 0.5 collective-permute-start.1
  101.8 2.3 %collective-permute-done.1.got_ref = bf16[4,32,32,128]{3,2,1,0:T(8,128)(2,1)S(1)} collective-permute-done((bf16[4,32,32,128]{3,2,1,0:T(8,128)(2,1)S(1)}, bf16[4,32,32,128]{3,2,1,0:T(8,128)(2,1)S(1)}, u32[]{:S(2)}, u32[]{:S(2)}) %collective-permute-start.1) | collective-permute-done | bytes 1048608 | tf_op jit(solution)/shard_map/ppermute | solution.py:455
  104.1 0.3 join.1
  104.4 0.0 copy-start
  104.4 45.3 %all_to_all.11 = bf16[128,96,128]{2,1,0:T(8,128)(2,1)S(1)} all-to-all(bf16[128,96,128]{2,1,0:T(8,128)(2,1)S(1)} %bitcast.8), channel_id=1, replica_groups=mesh['dp'=4,'ctx'=32] {'dp','ctx'}, dimensions={0} | all-to-all | bytes 6291456 | tf_op jit(solution)/shard_map/all_to_all | solution.py:466
  149.7 0.0 copy-done
  149.7 2.6 %unpack.1 = (bf16[128,4096]{1,0:T(8,128)(2,1)}, bf16[128,4096]{1,0:T(8,128)(2,1)}, bf16[128,512]{1,0:T(8,128)(2,1)}, bf16[128,512]{1,0:T(8,128)(2,1)}) custom-call(s32[1,128]{1,0:T(1,128)S(1)} %bitcast.11, bf16[2,2,2,16,96,128]{5,4,3,2,1,0:T(8,128)(2,1)S(1)} %bitcast.9), custom_call_target="tpu_custom_call" | custom-call | tf_op jit(solution)/shard_map/unpack/pallas_call | solution.py:159
Async XLA Ops:
  60.1 2.8 %collective-permute-start = (bf16[4,32,32,128]{3,2,1,0:T(8,128)(2,1)S(1)}, bf16[4,32,32,128]{3,2,1,0:T(8,128)(2,1)S(1)}, u32[]{:S(2)}, u32[]{:S(2)}) collective-permute-start(bf16[4,32,32,128]{3,2,1,0:T(8,128)(2,1)S(1)} %slice.4), channel_id=1, source_target_pairs={{0,32},{32,0},{64,96},{96,64},{1,33},{33,1},{65,97},{97,65},{2,34}... | collective-permute-start | bytes 3145736 | tf_op jit(solution)/shard_map/ppermute | solution.py:455
  101.4 2.7 %collective-permute-start.1 = (bf16[4,32,32,128]{3,2,1,0:T(8,128)(2,1)S(1)}, bf16[4,32,32,128]{3,2,1,0:T(8,128)(2,1)S(1)}, u32[]{:S(2)}, u32[]{:S(2)}) collective-permute-start(bf16[4,32,32,128]{3,2,1,0:T(8,128)(2,1)S(1)} %get-tuple-element.9), channel_id=1, source_target_pairs={{0,32},{32,0},{64,96},{96,64},{1,33},{33,1},{65,97},{97,65},{2,34}... | collective-permute-start | bytes 3145736 | tf_op jit(solution)/shard_map/ppermute | solution.py:455
  104.4 45.3 %copy-start = (s32[128]{0:T(128)S(1)}, s32[128]{0:T(128)}, u32[]{:S(2)}) copy-start(s32[128]{0:T(128)} %param.10) | copy-start | bytes 1540

commit v4 on v3

--- a/solution.py
+++ b/solution.py
@@ -19,6 +19,8 @@
 SEQ = 4096
 TQ = 256
 TK = 512
+PAD = TK - TQ
+TILES = SEQ // TQ
 
 IN_ROWS = 3 * SHARE + 8
 OUT_ROWS = 3 * SHARE
@@ -228,27 +230,35 @@
 
     def lay_out(c, carry):
         at = pl.ds(pl.multiple_of(c * TOK, TOK), TOK)
+        key_at = pl.ds(pl.multiple_of(c * TOK + PAD, TOK), TOK)
         mine = z_ref[:, c, 64:96, :].reshape(TOK, HEAD_DIM)
         theirs = other_ref[:, c].reshape(TOK, HEAD_DIM)
         key_tile = jnp.where(core == 0, mine, theirs)
         value_tile = jnp.where(core == 0, theirs, mine)
         d_tile = z_ref[:, c, SHARE : 2 * SHARE, :].reshape(TOK, HEAD_DIM)
         q_s[at, :] = z_ref[:, c, 0:SHARE, :].reshape(TOK, HEAD_DIM)
-        k_s[at, :] = key_tile
-        v_s[at, :] = value_tile
+        k_s[key_at, :] = key_tile
+        v_s[key_at, :] = value_tile
         d_s[at, :] = d_tile
-        kt_s[c] = key_tile.T
-        vt_s[c] = value_tile.T
+        kt_s[c + PAD // TOK] = key_tile.T
+        vt_s[c + PAD // TOK] = value_tile.T
         dt_s[c] = d_tile.T
         spot = c * TOK + lax.broadcasted_iota(jnp.int32, (TOK, HEAD_DIM), 0)
         early = spot < ends
-        qa_s[at, :] = jnp.where(used & ~early, NEG, 0.0).astype(jnp.bfloat16)
-        ka_s[at, :] = jnp.where(used & early, 1.0, 0.0).astype(jnp.bfloat16)
-        dk_s[at, :] = jnp.zeros((TOK, HEAD_DIM), jnp.float32)
-        dv_s[at, :] = jnp.zeros((TOK, HEAD_DIM), jnp.float32)
+        qa_s[at, :] = jnp.where((used & ~early) | (lane == DOCS), NEG, 0.0).astype(jnp.bfloat16)
+        ka_s[key_at, :] = jnp.where(used & early, 1.0, 0.0).astype(jnp.bfloat16)
+        dk_s[key_at, :] = jnp.zeros((TOK, HEAD_DIM), jnp.float32)
+        dv_s[key_at, :] = jnp.zeros((TOK, HEAD_DIM), jnp.float32)
         return carry
 
     lax.fori_loop(0, SEQ // TOK, lay_out, 0, unroll=4)
+    for pad_s in (k_s, v_s, dk_s, dv_s):
+        pad_s[:PAD, :] = jnp.zeros((PAD, HEAD_DIM), pad_s.dtype)
+    for n in range(PAD // TOK):
+        kt_s[n] = jnp.zeros((HEAD_DIM, TOK), jnp.bfloat16)
+        vt_s[n] = jnp.zeros((HEAD_DIM, TOK), jnp.bfloat16)
+    hidden = jnp.where(jnp.broadcast_to(lane, (PAD, HEAD_DIM)) == DOCS, 1.0, 0.0)
+    ka_s[:PAD, :] = hidden.astype(jnp.bfloat16)
 
     def doc_start(position):
         start = jnp.zeros_like(position)
@@ -257,11 +267,13 @@
         return start
 
     def chunks(i):
-        first_row = i * TQ
-        return doc_start(first_row) // TK, (first_row + TQ - 1) // TK + 1
-
-    def key_at(j):
-        return pl.ds(pl.multiple_of(j * TK, TK), TK)
+        return ((i + 1) * TQ - doc_start(i * TQ) + TK - 1) // TK
+
+    def key_at(i, t):
+        return pl.ds(pl.multiple_of(i * TQ - t * TK, TQ), TK)
+
+    def key_blocks(cols_s, i, t):
+        return side_by_side(cols_s, (i * TQ - t * TK) // TOK, TK // TOK)
 
     def query_at(i):
         return pl.ds(pl.multiple_of(i * TQ, TQ), TQ)
@@ -274,15 +286,18 @@
         sum_s[...] = jnp.zeros((8, TQ), jnp.float32)
         ot_s[...] = jnp.zeros((HEAD_DIM, TQ), jnp.float32)
 
-    def scores_of(i, j, p_s):
-        k_at, q_at = key_at(j), query_at(i)
+    def scores_of(i, t, last):
+        k_at, q_at = key_at(i, t), query_at(i)
         keys = jnp.concatenate([k_s[k_at, :], ka_s[k_at, :]], axis=1)
         scores = dot_nt(keys, jnp.concatenate([q_s[q_at, :], qa_s[q_at, :]], axis=1))
-        rows = i * TQ - j * TK + lax.broadcasted_iota(jnp.int32, (1, TQ), 1)
-        keys = lax.broadcasted_iota(jnp.int32, (TK, TQ), 0)
-        return jnp.where(keys <= rows, scores, NEG).reshape(tall)
-
-    def soften(scores, j, p_s, tops_s):
+        if last:
+            ahead = lax.broadcasted_iota(jnp.int32, (TQ, TQ), 0)
+            reach = lax.broadcasted_iota(jnp.int32, (TQ, TQ), 1)
+            own = jnp.where(ahead <= reach, scores[PAD:], NEG)
+            scores = jnp.concatenate([scores[:PAD], own], axis=0)
+        return scores.reshape(tall)
+
+    def soften(scores, i, t, p_s, tops_s):
         before = top_s[...]
         here = jnp.max(jnp.max(scores, axis=0), axis=0, keepdims=True)
         top = jnp.maximum(before, jnp.broadcast_to(here, (8, TQ)))
@@ -290,33 +305,33 @@
         fade = jnp.exp2((before - top) * to_exp2)
         sum_s[...] = sum_s[...] * fade + jnp.sum(part, axis=0)
         top_s[...] = top
-        tops_s[j] = top
+        tops_s[t] = top
         part = part.reshape(TK, TQ)
-        p_s[key_at(j), :] = part
+        p_s[key_at(i, t), :] = part
         return part.astype(jnp.bfloat16), fade
 
-    def add_out(j, part, fade):
+    def add_out(i, t, part, fade):
         faded = (ot_s[...].reshape(HEAD_DIM // 8, 8, TQ) * fade).reshape(HEAD_DIM, TQ)
-        ot_s[...] = faded + dot(side_by_side(vt_s, j * (TK // TOK), TK // TOK), part)
-
-    def forward_step(i, j, p_s, tops_s):
-        part, fade = soften(scores_of(i, j, p_s), j, p_s, tops_s)
-        add_out(j, part, fade)
-
-    def both_steps(i, j, p_s, tops_s, i_now, j_now, p_now, tops_now, rows_now):
-        scores = scores_of(i, j, p_s)
-        k_at, q_at = key_at(j_now), query_at(i_now)
+        ot_s[...] = faded + dot(key_blocks(vt_s, i, t), part)
+
+    def forward_step(i, t, last, p_s, tops_s):
+        part, fade = soften(scores_of(i, t, last), i, t, p_s, tops_s)
+        add_out(i, t, part, fade)
+
+    def both_steps(i, t, last, p_s, tops_s, i_now, p_now, tops_now, rows_now):
+        scores = scores_of(i, t, last)
+        k_at, q_at = key_at(i_now, t), query_at(i_now)
         dprobs = dot_nt(v_s[k_at, :], d_s[q_at, :]).reshape(tall)
-        share = jnp.exp2((tops_now[j_now] - rows_now[0]) * to_exp2) * rows_now[1]
+        share = jnp.exp2((tops_now[t] - rows_now[0]) * to_exp2) * rows_now[1]
         held = p_now[k_at, :].reshape(tall)
         weights = (held * share).reshape(TK, TQ).astype(jnp.bfloat16)
         dv_s[k_at, :] += dot(weights, d_s[q_at, :])
-        part, fade = soften(scores, j, p_s, tops_s)
+        part, fade = soften(scores, i, t, p_s, tops_s)
         dscore = (held * (share * scaling)) * (dprobs - rows_now[2])
         dscore = dscore.reshape(TK, TQ).astype(jnp.bfloat16)
         dk_s[k_at, :] += dot(dscore, q_s[q_at, :])
-        qg_s[...] += dot(side_by_side(kt_s, j_now * (TK // TOK), TK // TOK), dscore)
-        add_out(j, part, fade)
+        qg_s[...] += dot(key_blocks(kt_s, i_now, t), dscore)
+        add_out(i, t, part, fade)
 
     def forward_end(i, rows_s):
         share = 1.0 / jnp.sum(sum_s[...], axis=0, keepdims=True)
@@ -332,9 +347,9 @@
             o_ref[:, i * (TQ // TOK) + n, 0:32] = tile
         clear_forward()
 
-    def gradient_step(i, j, p_s, tops_s, rows_s):
-        k_at, q_at = key_at(j), query_at(i)
-        share = jnp.exp2((tops_s[j] - rows_s[0]) * to_exp2) * rows_s[1]
+    def gradient_step(i, t, p_s, tops_s, rows_s):
+        k_at, q_at = key_at(i, t), query_at(i)
+        share = jnp.exp2((tops_s[t] - rows_s[0]) * to_exp2) * rows_s[1]
         dprobs = dot_nt(v_s[k_at, :], d_s[q_at, :]).reshape(tall)
         part = p_s[k_at, :].reshape(tall)
         weights = (part * share).reshape(TK, TQ).astype(jnp.bfloat16)
@@ -342,7 +357,7 @@
         dscore = (part * (share * scaling)) * (dprobs - rows_s[2])
         dscore = dscore.reshape(TK, TQ).astype(jnp.bfloat16)
         dk_s[k_at, :] += dot(dscore, q_s[q_at, :])
-        qg_s[...] += dot(side_by_side(kt_s, j * (TK // TOK), TK // TOK), dscore)
+        qg_s[...] += dot(key_blocks(kt_s, i, t), dscore)
 
     def gradient_end(i):
         grad_rows = qg_s[...].astype(jnp.bfloat16).T
@@ -355,37 +370,35 @@
     odd = (p_odd, tops_odd, rows_odd)
 
     def stage(i_next, ahead, i_now, behind):
-        now_lo, now_hi = chunks(i_now)
-        next_lo, next_hi = chunks(jnp.minimum(i_next, SEQ // TQ - 1))
-        next_n = jnp.where(i_next < SEQ // TQ, next_hi - next_lo, 0)
-        now_n = now_hi - now_lo
+        now_n = chunks(i_now)
+        next_n = jnp.where(i_next < TILES, chunks(jnp.minimum(i_next, TILES - 1)), 0)
         both = jnp.minimum(next_n, now_n)
 
         def together(t, carry):
-            both_steps(i_next, next_lo + t, *ahead[:2], i_now, now_lo + t, *behind)
+            both_steps(i_next, t, False, *ahead[:2], i_now, *behind)
             return carry
 
         def ahead_only(t, carry):
-            forward_step(i_next, next_lo + t, *ahead[:2])
+            forward_step(i_next, t, False, *ahead[:2])
             return carry
 
         def behind_only(t, carry):
-            gradient_step(i_now, now_lo + t, *behind)
+            gradient_step(i_now, t, *behind)
             return carry
 
-        lax.fori_loop(0, both, together, 0)
-        lax.fori_loop(both, next_n, ahead_only, 0)
+        @pl.when(i_next < TILES)
+        def _():
+            both_steps(i_next, 0, True, *ahead[:2], i_now, *behind)
+            lax.fori_loop(1, both, together, 0)
+            lax.fori_loop(both, next_n, ahead_only, 0)
+            forward_end(i_next, ahead[2])
+
         lax.fori_loop(both, now_n, behind_only, 0)
-
-        @pl.when(i_next < SEQ // TQ)
-        def _():
-            forward_end(i_next, ahead[2])
-
         gradient_end(i_now)
 
     clear_forward()
     qg_s[...] = jnp.zeros((HEAD_DIM, TQ), jnp.float32)
-    forward_step(0, 0, *even[:2])
+    forward_step(0, 0, True, *even[:2])
     forward_end(0, rows_even)
 
     def two_stages(m, carry):
@@ -393,10 +406,10 @@
         stage(2 * m + 2, even, 2 * m + 1, odd)
         return carry
 
-    lax.fori_loop(0, SEQ // TQ // 2, two_stages, 0)
+    lax.fori_loop(0, TILES // 2, two_stages, 0)
 
     def give_back(c, carry):
-        at = pl.ds(pl.multiple_of(c * TOK, TOK), TOK)
+        at = pl.ds(pl.multiple_of(c * TOK + PAD, TOK), TOK)
         k_part = dk_s[at, :].astype(jnp.bfloat16)
         v_part = dv_s[at, :].astype(jnp.bfloat16)
         keep_ref[:, c] = jnp.where(core == 0, k_part, v_part).reshape(4, SHARE, HEAD_DIM)
@@ -408,7 +421,9 @@
 
 def attention(z, other):
     tall = pltpu.VMEM((SEQ, HEAD_DIM), jnp.bfloat16)
+    keys = pltpu.VMEM((SEQ + PAD, HEAD_DIM), jnp.bfloat16)
     flat = pltpu.VMEM((SEQ // TOK, TOK, HEAD_DIM), jnp.bfloat16)
+    key_cols = pltpu.VMEM(((SEQ + PAD) // TOK, TOK, HEAD_DIM), jnp.bfloat16)
     whole = pl.BlockSpec(memory_space=pltpu.VMEM)
     part = jax.ShapeDtypeStruct((4, 32, SHARE, HEAD_DIM), jnp.bfloat16)
     return pl.pallas_call(
@@ -416,12 +431,11 @@
         in_specs=[whole, whole],
         out_specs=[whole, whole, whole],
         out_shape=[jax.ShapeDtypeStruct((4, 32, 2 * SHARE, HEAD_DIM), jnp.bfloat16), part, part],
-        scratch_shapes=[tall] * 6
-        + [flat] * 3
-        + [pltpu.VMEM((SEQ, TQ), jnp.float32)] * 2
+        scratch_shapes=[tall, tall, tall, keys, keys, keys, flat, key_cols, key_cols]
+        + [pltpu.VMEM((SEQ + PAD, TQ), jnp.float32)] * 2
         + [pltpu.VMEM((SEQ // TK, 8, TQ), jnp.float32)] * 2
         + [pltpu.VMEM((3, 8, TQ), jnp.float32)] * 2
-        + [pltpu.VMEM((SEQ, HEAD_DIM), jnp.float32)] * 2
+        + [pltpu.VMEM((SEQ + PAD, HEAD_DIM), jnp.float32)] * 2
         + [pltpu.VMEM((HEAD_DIM, TQ), jnp.float32)] * 2
         + [pltpu.VMEM((8, TQ), jnp.float32)] * 2,
         compiler_params=pltpu.CompilerParams(vmem_limit_bytes=36 << 20),

time: 151 us -> 147 us (0.974); the launches traced: 152 us -> 147 us
  Pallas kernels: 44.5 us -> 38.8 us
    pallas_call x1, Pallas kernels: 38.5 us -> 32.7 us  [attention(): pl.pallas_call(attention_kernel, in_specs=[whole, whole], out_specs=[whol...]
where the time goes in v4:
time: 147 us
  blocking collectives  102 us (69%)
  Pallas kernels  38.8 us (26%)
  waiting for transfers between devices  4.58 us (3%)
    all_to_all x1, blocking collectives, on_device(): lax.all_to_all(sent.reshape(TOK, IN_ROWS, HEAD_DIM), ('dp', 'ctx'), split...  56.2 us
    all_to_all x1, blocking collectives, on_device(): lax.all_to_all(done.reshape(TOK, OUT_ROWS, HEAD_DIM), ('dp', 'ctx'), spli...  45.3 us
    pallas_call x1, Pallas kernels, attention(): pl.pallas_call(attention_kernel, in_specs=[whole, whole], out_specs=[whol...  32.7 us
    ppermute x2, waiting for transfers between devices, to_other_core(): return lax.ppermute(x, 'dp', [(0, 1), (1, 0), (2, 3), (3, 2)])  4.58 us
    pallas_call x1, Pallas kernels, pack(): pl.pallas_call(pack_kernel, in_specs=[outside] * 6, out_specs=pl.BlockSpe...  3.14 us
  transfers between devices with their start and end apart: 2, of which 2 were waited for; matrix products, arithmetic and copies ran while one was open for 0% of the time, Pallas kernels for 0%

profile of v4, /device:TPU:1, one launch (start us, length us, event | category | flops | bytes accessed | tf_op | source)
XLA Modules:
  0.0 146.6 jit_solution(6068782022815210554)
XLA Ops:
  0.6 3.1 %pack.1 = bf16[2,2,2,16,104,128]{5,4,3,2,1,0:T(8,128)(2,1)S(1)} custom-call(s32[1,128]{1,0:T(1,128)} %bitcast.10, s32[1,128]{1,0:T(1,128)} %seg_hbm.1, bf16[128,4096]{1,0:T(8,128)(2,1)} %q_hbm.1, bf16[128,4096]{1,0:T(8,128)(2,1)} %d_hbm.1, bf16[128,512]{1,0:T(8,128)(2,1)} %k_hbm.1, bf16[128,512]{1,0:T(8,128)(2,1)} %v_hbm.1), custom_call_target="tpu_custom_call" | custom-call | tf_op jit(solution)/shard_map/pack/pallas_call | solution.py:116
  3.8 56.2 %all_to_all.10 = bf16[128,104,128]{2,1,0:T(8,128)(2,1)S(1)} all-to-all(bf16[128,104,128]{2,1,0:T(8,128)(2,1)S(1)} %bitcast.7), channel_id=1, replica_groups=mesh['dp'=4,'ctx'=32] {'dp','ctx'}, dimensions={0} | all-to-all | bytes 6815744 | tf_op jit(solution)/shard_map/all_to_all | solution.py:474
  60.0 0.1 slice.4
  60.1 0.5 collective-permute-start
  60.6 2.3 %collective-permute-done.other_ref = bf16[4,32,32,128]{3,2,1,0:T(8,128)(2,1)S(1)} collective-permute-done((bf16[4,32,32,128]{3,2,1,0:T(8,128)(2,1)S(1)}, bf16[4,32,32,128]{3,2,1,0:T(8,128)(2,1)S(1)}, u32[]{:S(2)}, u32[]{:S(2)}) %collective-permute-start) | collective-permute-done | bytes 1048608 | tf_op jit(solution)/shard_map/ppermute | solution.py:469
  62.9 32.7 %attention.1 = (bf16[4,32,64,128]{3,2,1,0:T(8,128)(2,1)S(1)}, bf16[4,32,32,128]{3,2,1,0:T(8,128)(2,1)S(1)}, bf16[4,32,32,128]{3,2,1,0:T(8,128)(2,1)S(1)}) custom-call(bf16[4,32,104,128]{3,2,1,0:T(8,128)(2,1)S(1)} %bitcast.6, bf16[4,32,32,128]{3,2,1,0:T(8,128)(2,1)S(1)} %collective-permute-done.other_ref), custom_call_target="tpu_custom_call" | custom-call | tf_op jit(solution)/shard_map/attention/pallas_call | solution.py:429
  95.6 0.4 collective-permute-start.1
  96.1 2.3 %collective-permute-done.1.got_ref = bf16[4,32,32,128]{3,2,1,0:T(8,128)(2,1)S(1)} collective-permute-done((bf16[4,32,32,128]{3,2,1,0:T(8,128)(2,1)S(1)}, bf16[4,32,32,128]{3,2,1,0:T(8,128)(2,1)S(1)}, u32[]{:S(2)}, u32[]{:S(2)}) %collective-permute-start.1) | collective-permute-done | bytes 1048608 | tf_op jit(solution)/shard_map/ppermute | solution.py:469
  98.4 0.3 join.1
  98.7 0.0 copy-start
  98.7 45.3 %all_to_all.11 = bf16[128,96,128]{2,1,0:T(8,128)(2,1)S(1)} all-to-all(bf16[128,96,128]{2,1,0:T(8,128)(2,1)S(1)} %bitcast.8), channel_id=1, replica_groups=mesh['dp'=4,'ctx'=32] {'dp','ctx'}, dimensions={0} | all-to-all | bytes 6291456 | tf_op jit(solution)/shard_map/all_to_all | solution.py:480
  144.0 0.0 copy-done
  144.0 2.6 %unpack.1 = (bf16[128,4096]{1,0:T(8,128)(2,1)}, bf16[128,4096]{1,0:T(8,128)(2,1)}, bf16[128,512]{1,0:T(8,128)(2,1)}, bf16[128,512]{1,0:T(8,128)(2,1)}) custom-call(s32[1,128]{1,0:T(1,128)S(1)} %bitcast.11, bf16[2,2,2,16,96,128]{5,4,3,2,1,0:T(8,128)(2,1)S(1)} %bitcast.9), custom_call_target="tpu_custom_call" | custom-call | tf_op jit(solution)/shard_map/unpack/pallas_call | solution.py:161
Async XLA Ops:
  60.1 2.8 %collective-permute-start = (bf16[4,32,32,128]{3,2,1,0:T(8,128)(2,1)S(1)}, bf16[4,32,32,128]{3,2,1,0:T(8,128)(2,1)S(1)}, u32[]{:S(2)}, u32[]{:S(2)}) collective-permute-start(bf16[4,32,32,128]{3,2,1,0:T(8,128)(2,1)S(1)} %slice.4), channel_id=1, source_target_pairs={{0,32},{32,0},{64,96},{96,64},{1,33},{33,1},{65,97},{97,65},{2,34}... | collective-permute-start | bytes 3145736 | tf_op jit(solution)/shard_map/ppermute | solution.py:469
  95.6 2.7 %collective-permute-start.1 = (bf16[4,32,32,128]{3,2,1,0:T(8,128)(2,1)S(1)}, bf16[4,32,32,128]{3,2,1,0:T(8,128)(2,1)S(1)}, u32[]{:S(2)}, u32[]{:S(2)}) collective-permute-start(bf16[4,32,32,128]{3,2,1,0:T(8,128)(2,1)S(1)} %get-tuple-element.9), channel_id=1, source_target_pairs={{0,32},{32,0},{64,96},{96,64},{1,33},{33,1},{65,97},{97,65},{2,34}... | collective-permute-start | bytes 3145736 | tf_op jit(solution)/shard_map/ppermute | solution.py:469
  98.7 45.3 %copy-start = (s32[128]{0:T(128)S(1)}, s32[128]{0:T(128)}, u32[]{:S(2)}) copy-start(s32[128]{0:T(128)} %param.10) | copy-start | bytes 1540
